TPU v7x, 8 devices: a whole 2x2x1 slice. The times are simulated.
8 devices in a mesh: data: 1 (over z), stage: 8 (over y, x, core).
Axes of the slice: x: 2, y: 2, z: 1, core: 2. Of those that a mesh axis runs over, the one named last changes fastest.
Arguments:
- acts_in: bfloat16 [8, 2048, 768], P(('data', 'stage'))
- grad_out: bfloat16 [8, 2048, 768], P(('data', 'stage'))
- w_up_a: bfloat16 [8, 768, 3072], P('stage')
- w_down_a: bfloat16 [8, 3072, 768], P('stage')
- w_up_b: bfloat16 [8, 768, 768], P('stage')
- w_down_b: bfloat16 [8, 768, 768], P('stage')
Outputs:
- output 1: bfloat16 [8, 2048, 768], P(('data', 'stage'))
- output 2: bfloat16 [8, 2048, 768], P(('data', 'stage'))
- output 3: float32 [8, 768, 3072], P(('data', 'stage'))
- output 4: float32 [8, 3072, 768], P(('data', 'stage'))
- output 5: float32 [8, 768, 768], P(('data', 'stage'))
- output 6: float32 [8, 768, 768], P(('data', 'stage'))
All inputs are finite; a program needn't handle non-finite values.
Results may differ from a plain program's by a relative error of at most 0.02.
Values are sent between devices in bfloat16 or wider.
A program may use at most 1 GiB of HBM per device.

v0:
```python
import jax
import jax.numpy as jnp
from jax import lax
from jax.sharding import PartitionSpec as P


def layer_forward(hidden, w_up, w_down):
    pre_act = jnp.dot(hidden, w_up, preferred_element_type=jnp.float32)
    gelu_out = jax.nn.gelu(pre_act).astype(jnp.bfloat16)
    resid_delta = jnp.dot(gelu_out, w_down, preferred_element_type=jnp.float32)
    return (hidden.astype(jnp.float32) + resid_delta).astype(jnp.bfloat16)


def layer_backward(hidden, w_up, w_down, grad_next):
    pre_act = jnp.dot(hidden, w_up, preferred_element_type=jnp.float32)
    gelu_val, gelu_pull = jax.vjp(jax.nn.gelu, pre_act)
    gelu_out = gelu_val.astype(jnp.bfloat16)
    dw_down = jnp.einsum('tf,td->fd', gelu_out, grad_next, preferred_element_type=jnp.float32)
    d_gelu = jnp.einsum('td,fd->tf', grad_next, w_down, preferred_element_type=jnp.float32)
    d_pre = gelu_pull(d_gelu)[0].astype(jnp.bfloat16)
    dw_up = jnp.einsum('td,tf->df', hidden, d_pre, preferred_element_type=jnp.float32)
    back_prod = jnp.einsum('tf,df->td', d_pre, w_up, preferred_element_type=jnp.float32)
    grad_prev = (grad_next.astype(jnp.float32) + back_prod).astype(jnp.bfloat16)
    return grad_prev, dw_up, dw_down


def pair_forward(hidden, pair_weights):
    up_a, down_a, up_b, down_b = pair_weights
    mid_hidden = layer_forward(hidden, up_a, down_a)
    return layer_forward(mid_hidden, up_b, down_b), (hidden, mid_hidden)


def pair_backward(grad_next, step_in):
    (hidden, mid_hidden), (up_a, down_a, up_b, down_b) = step_in
    grad_mid, dw_up_b, dw_down_b = layer_backward(mid_hidden, up_b, down_b, grad_next)
    grad_prev, dw_up_a, dw_down_a = layer_backward(hidden, up_a, down_a, grad_mid)
    return grad_prev, (dw_up_a, dw_down_a, dw_up_b, dw_down_b)


def gather_round(local_rows, round_idx):
    return tuple(lax.all_gather(weight[round_idx], 'stage') for weight in local_rows)


def solution(mesh):
    tok_spec = P(('data', 'stage'))
    row_spec = P('stage')

    def device_body(acts_in, grad_out, w_up_a, w_down_a, w_up_b, w_down_b):
        n_micro, tokens, model_width = acts_in.shape
        local_rows = (w_up_a, w_down_a, w_up_b, w_down_b)
        num_rounds = w_up_a.shape[0]
        hidden = acts_in.reshape(n_micro * tokens, model_width)
        saved_acts = []
        for round_idx in range(num_rounds):
            hidden, round_saved = lax.scan(pair_forward, hidden, gather_round(local_rows, round_idx))
            saved_acts.append(round_saved)
        grad_h = grad_out.reshape(n_micro * tokens, model_width)
        round_grads = []
        for round_idx in reversed(range(num_rounds)):
            round_weights = gather_round(local_rows, round_idx)
            grad_h, pair_grads = lax.scan(pair_backward, grad_h, (saved_acts[round_idx], round_weights), reverse=True)
            round_grads.append(tuple(lax.psum_scatter(grad_stack, 'stage', scatter_dimension=0, tiled=True) for grad_stack in pair_grads))
        round_grads = round_grads[::-1]
        weight_grads = tuple(jnp.concatenate([round_set[slot_idx] for round_set in round_grads], axis=0) for slot_idx in range(4))
        return (hidden.reshape(acts_in.shape), grad_h.reshape(acts_in.shape)) + weight_grads

    return jax.shard_map(device_body, mesh=mesh, in_specs=(tok_spec, tok_spec, row_spec, row_spec, row_spec, row_spec), out_specs=(tok_spec,) * 6, check_vma=False)
```

profile of v0, /device:TPU:0, one launch (start us, length us, event | category | flops | bytes accessed | tf_op | source)
XLA Modules:
  0.0 2969.4 jit_solution(2849151977791743229)
XLA Ops:
  10.0 55.6 %all-gather.9.cloned.1.call-done = bf16[8,768,768]{2,1,0:T(8,128)(2,1)} async-done(((bf16[1,768,768]{2,1,0:T(8,128)(2,1)}), bf16[8,768,768]{2,1,0:T(8,128)(2,1)}) %all-gather.9.cloned.1.call-update) | async-done | bytes 9437200 | tf_op jit(solution)/shard_map/all_gather | solution.py:41
  65.6 54.8 %all-gather.11.cloned.1.call-done = bf16[8,768,768]{2,1,0:T(8,128)(2,1)} async-done(((bf16[1,768,768]{2,1,0:T(8,128)(2,1)}), bf16[8,768,768]{2,1,0:T(8,128)(2,1)}) %all-gather.11.cloned.1.call-update) | async-done | bytes 9437200 | tf_op jit(solution)/shard_map/all_gather | solution.py:41
  120.4 175.9 %all-gather.5.cloned.1.call-done = bf16[8,768,3072]{2,1,0:T(8,128)(2,1)} async-done(((bf16[1,768,3072]{2,1,0:T(8,128)(2,1)}), bf16[8,768,3072]{2,1,0:T(8,128)(2,1)}) %all-gather.5.cloned.1.call-update) | async-done | bytes 37748752 | tf_op jit(solution)/shard_map/all_gather | solution.py:41
  296.2 175.7 %all-gather.7.cloned.1.call-done = bf16[8,3072,768]{2,1,0:T(8,128)(2,1)} async-done(((bf16[1,3072,768]{2,1,0:T(8,128)(2,1)}), bf16[8,3072,768]{2,1,0:T(8,128)(2,1)}) %all-gather.7.cloned.1.call-update) | async-done | bytes 37748752 | tf_op jit(solution)/shard_map/all_gather | solution.py:41
  472.0 337.8 %while.37 = (s32[]{:T(128)}, bf16[2048,768]{1,0:T(8,128)(2,1)S(1)}, bf16[8,2048,768]{2,1,0:T(8,128)(2,1)}, bf16[8,2048,768]{2,1,0:T(8,128)(2,1)}, bf16[8,768,307...) while((s32[]{:T(128)}, bf16[2048,768]{1,0:T(8,128)(2,1)S(1)}, ...), condition=%wide.region_1.2_spmd, body=%wide.region_0.1_spmd.sunk | while | flops 24239407104 | bytes 40110696 | solution.py:55
  473.8 31.8 %bitcast_dynamic-update-slice_fusion.12 = (bf16[8,2048,768]{2,1,0:T(8,128)(2,1)}, bf16[2048,768]{1,0:T(8,128)(2,1)}) fusion(bf16[8,2048,768]{2,1,0:T(8,128)(2,1)} %get-tuple-element.511, s32[]{:T(128)S(6)} %copy.35, bf16[8,3072,768]{2,1,0:T(8,128)(2,1)} %get-tuple-element.522, bf16[2048,768]{1,0:T(8,128)(2,1)S(1)} %get-tuple-element.509, ...), kind=kOutput, calls=%fused_computation.25.clone.1 | convolution fusion | flops 19388694528 | bytes 22021632 | tf_op jit(solution)/shard_map/while/body/eval_jaxpr/dot_general | solution.py:10
  516.0 31.8 %bitcast_dynamic-update-slice_fusion.12 = (bf16[8,2048,768]{2,1,0:T(8,128)(2,1)}, bf16[2048,768]{1,0:T(8,128)(2,1)}) fusion(bf16[8,2048,768]{2,1,0:T(8,128)(2,1)} %get-tuple-element.511, s32[]{:T(128)S(6)} %copy.35, bf16[8,3072,768]{2,1,0:T(8,128)(2,1)} %get-tuple-element.522, bf16[2048,768]{1,0:T(8,128)(2,1)S(1)} %get-tuple-element.509, ...), kind=kOutput, calls=%fused_computation.25.clone.1 | convolution fusion | flops 19388694528 | bytes 22021632 | tf_op jit(solution)/shard_map/while/body/eval_jaxpr/dot_general | solution.py:10
  558.1 31.8 %bitcast_dynamic-update-slice_fusion.12 = (bf16[8,2048,768]{2,1,0:T(8,128)(2,1)}, bf16[2048,768]{1,0:T(8,128)(2,1)}) fusion(bf16[8,2048,768]{2,1,0:T(8,128)(2,1)} %get-tuple-element.511, s32[]{:T(128)S(6)} %copy.35, bf16[8,3072,768]{2,1,0:T(8,128)(2,1)} %get-tuple-element.522, bf16[2048,768]{1,0:T(8,128)(2,1)S(1)} %get-tuple-element.509, ...), kind=kOutput, calls=%fused_computation.25.clone.1 | convolution fusion | flops 19388694528 | bytes 22021632 | tf_op jit(solution)/shard_map/while/body/eval_jaxpr/dot_general | solution.py:10
  600.3 31.8 %bitcast_dynamic-update-slice_fusion.12 = (bf16[8,2048,768]{2,1,0:T(8,128)(2,1)}, bf16[2048,768]{1,0:T(8,128)(2,1)}) fusion(bf16[8,2048,768]{2,1,0:T(8,128)(2,1)} %get-tuple-element.511, s32[]{:T(128)S(6)} %copy.35, bf16[8,3072,768]{2,1,0:T(8,128)(2,1)} %get-tuple-element.522, bf16[2048,768]{1,0:T(8,128)(2,1)S(1)} %get-tuple-element.509, ...), kind=kOutput, calls=%fused_computation.25.clone.1 | convolution fusion | flops 19388694528 | bytes 22021632 | tf_op jit(solution)/shard_map/while/body/eval_jaxpr/dot_general | solution.py:10
  642.5 31.8 %bitcast_dynamic-update-slice_fusion.12 = (bf16[8,2048,768]{2,1,0:T(8,128)(2,1)}, bf16[2048,768]{1,0:T(8,128)(2,1)}) fusion(bf16[8,2048,768]{2,1,0:T(8,128)(2,1)} %get-tuple-element.511, s32[]{:T(128)S(6)} %copy.35, bf16[8,3072,768]{2,1,0:T(8,128)(2,1)} %get-tuple-element.522, bf16[2048,768]{1,0:T(8,128)(2,1)S(1)} %get-tuple-element.509, ...), kind=kOutput, calls=%fused_computation.25.clone.1 | convolution fusion | flops 19388694528 | bytes 22021632 | tf_op jit(solution)/shard_map/while/body/eval_jaxpr/dot_general | solution.py:10
  684.7 31.8 %bitcast_dynamic-update-slice_fusion.12 = (bf16[8,2048,768]{2,1,0:T(8,128)(2,1)}, bf16[2048,768]{1,0:T(8,128)(2,1)}) fusion(bf16[8,2048,768]{2,1,0:T(8,128)(2,1)} %get-tuple-element.511, s32[]{:T(128)S(6)} %copy.35, bf16[8,3072,768]{2,1,0:T(8,128)(2,1)} %get-tuple-element.522, bf16[2048,768]{1,0:T(8,128)(2,1)S(1)} %get-tuple-element.509, ...), kind=kOutput, calls=%fused_computation.25.clone.1 | convolution fusion | flops 19388694528 | bytes 22021632 | tf_op jit(solution)/shard_map/while/body/eval_jaxpr/dot_general | solution.py:10
  726.9 31.9 %bitcast_dynamic-update-slice_fusion.12 = (bf16[8,2048,768]{2,1,0:T(8,128)(2,1)}, bf16[2048,768]{1,0:T(8,128)(2,1)}) fusion(bf16[8,2048,768]{2,1,0:T(8,128)(2,1)} %get-tuple-element.511, s32[]{:T(128)S(6)} %copy.35, bf16[8,3072,768]{2,1,0:T(8,128)(2,1)} %get-tuple-element.522, bf16[2048,768]{1,0:T(8,128)(2,1)S(1)} %get-tuple-element.509, ...), kind=kOutput, calls=%fused_computation.25.clone.1 | convolution fusion | flops 19388694528 | bytes 22021632 | tf_op jit(solution)/shard_map/while/body/eval_jaxpr/dot_general | solution.py:10
  769.2 31.8 %bitcast_dynamic-update-slice_fusion.12 = (bf16[8,2048,768]{2,1,0:T(8,128)(2,1)}, bf16[2048,768]{1,0:T(8,128)(2,1)}) fusion(bf16[8,2048,768]{2,1,0:T(8,128)(2,1)} %get-tuple-element.511, s32[]{:T(128)S(6)} %copy.35, bf16[8,3072,768]{2,1,0:T(8,128)(2,1)} %get-tuple-element.522, bf16[2048,768]{1,0:T(8,128)(2,1)S(1)} %get-tuple-element.509, ...), kind=kOutput, calls=%fused_computation.25.clone.1 | convolution fusion | flops 19388694528 | bytes 22021632 | tf_op jit(solution)/shard_map/while/body/eval_jaxpr/dot_general | solution.py:10
  825.9 23.9 broadcast_in_dim.57
  849.8 23.9 broadcast_in_dim.56
  873.7 1012.4 %while.38 = (s32[]{:T(128)}, bf16[2048,768]{1,0:T(8,128)(2,1)S(1)}, f32[8,768,3072]{2,1,0:T(8,128)}, f32[8,3072,768]{2,1,0:T(8,128)}, f32[8,768,768]{2,1,0:T(8,1...) while((s32[]{:T(128)}, bf16[2048,768]{1,0:T(8,128)(2,1)S(1)}, ...), condition=%wide.region_3.4_spmd, body=%wide.region_2.3_spmd.sunk | while | flops 60635480064 | bytes 220598432 | solution.py:61
  941.6 27.1 fusion.188
  1065.1 27.1 fusion.188
  1106.6 20.9 bitcast_dynamic-update-slice_fusion.15
  1188.9 27.1 fusion.188
  1230.4 21.0 bitcast_dynamic-update-slice_fusion.15
  1312.6 27.1 fusion.188
  1354.1 20.9 bitcast_dynamic-update-slice_fusion.15
  1436.3 27.1 fusion.188
  1559.9 27.1 fusion.188
  1683.8 27.1 fusion.188
  1725.3 20.9 bitcast_dynamic-update-slice_fusion.15
  1807.6 27.1 fusion.188
  1889.8 113.5 %reduce-scatter.11.cloned.1.call-done = f32[1,768,768]{2,1,0:T(8,128)} async-done(((f32[8,768,768]{2,1,0:T(8,128)}), f32[1,768,768]{2,1,0:T(8,128)}) %reduce-scatter.11.cloned.1.call-update) | async-done | bytes 2359312 | tf_op jit(solution)/shard_map/reduce_scatter | solution.py:62
  2003.3 121.1 %reduce-scatter.9.cloned.1.call-done = f32[1,768,768]{2,1,0:T(8,128)} async-done(((f32[8,768,768]{2,1,0:T(8,128)}), f32[1,768,768]{2,1,0:T(8,128)}) %reduce-scatter.9.cloned.1.call-update) | async-done | bytes 2359312 | tf_op jit(solution)/shard_map/reduce_scatter | solution.py:62
  2124.4 418.9 %reduce-scatter.5.cloned.1.call-done = f32[1,768,3072]{2,1,0:T(8,128)} async-done(((f32[8,768,3072]{2,1,0:T(8,128)}), f32[1,768,3072]{2,1,0:T(8,128)}) %reduce-scatter.5.cloned.1.call-update) | async-done | bytes 9437200 | tf_op jit(solution)/shard_map/reduce_scatter | solution.py:62
  2543.3 418.9 %reduce-scatter.7.cloned.1.call-done = f32[1,3072,768]{2,1,0:T(8,128)} async-done(((f32[8,3072,768]{2,1,0:T(8,128)}), f32[1,3072,768]{2,1,0:T(8,128)}) %reduce-scatter.7.cloned.1.call-update) | async-done | bytes 9437200 | tf_op jit(solution)/shard_map/reduce_scatter | solution.py:62
  (112 shorter events, 794.1 us)
Async XLA Ops:
  7.2 58.4 %all-gather.9.cloned.1.call-start = ((), (), s32[]{:S(2)}) async-start(), calls=%async_computation.6 | async-start | bytes 10616832 | tf_op jit(solution)/shard_map/all_gather | solution.py:41
  7.2 464.8 %copy-start.1 = (bf16[1,2048,768]{2,1,0:T(8,128)(2,1)S(1)}, bf16[1,2048,768]{2,1,0:T(8,128)(2,1)}, u32[]{:S(2)}) copy-start(bf16[1,2048,768]{2,1,0:T(8,128)(2,1)} %param.10) | copy-start | bytes 9437188
  7.9 112.5 %all-gather.11.cloned.1.call-start = ((), (), s32[]{:S(2)}) async-start(), calls=%async_computation.7 | async-start | bytes 10616832 | tf_op jit(solution)/shard_map/all_gather | solution.py:41
  8.6 287.6 %all-gather.5.cloned.1.call-start = ((), (), s32[]{:S(2)}) async-start(), calls=%async_computation.4 | async-start | bytes 42467328 | tf_op jit(solution)/shard_map/all_gather | solution.py:41
  9.4 462.6 %all-gather.7.cloned.1.call-start = ((), (), s32[]{:S(2)}) async-start(), calls=%async_computation.5 | async-start | bytes 42467328 | tf_op jit(solution)/shard_map/all_gather | solution.py:41
  10.0 1993.4 %reduce-scatter.11.cloned.1.call-start = ((), (), s32[]{:S(2)}) async-start(), calls=%async_computation.11 | async-start | bytes 21233664 | tf_op jit(solution)/shard_map/reduce_scatter | solution.py:62
  809.8 8.0 copy-start
  849.8 23.9 copy-start.3
  1886.1 1.7 copy-start.2
  1887.8 236.6 %reduce-scatter.9.cloned.1.call-start = ((), (), s32[]{:S(2)}) async-start(), calls=%async_computation.10 | async-start | bytes 21233664 | tf_op jit(solution)/shard_map/reduce_scatter | solution.py:62
  1888.3 655.0 %reduce-scatter.5.cloned.1.call-start = ((), (), s32[]{:S(2)}) async-start(), calls=%async_computation.8 | async-start | bytes 84934656 | tf_op jit(solution)/shard_map/reduce_scatter | solution.py:62
  1889.1 1073.1 %reduce-scatter.7.cloned.1.call-start = ((), (), s32[]{:S(2)}) async-start(), calls=%async_computation.9 | async-start | bytes 84934656 | tf_op jit(solution)/shard_map/reduce_scatter | solution.py:62
Sparse Core Ops, SparseCore 0:
  9.8 55.7 all-gather.8
  67.4 52.9 all-gather.10
  122.2 173.9 all-gather.4
  297.9 173.9 all-gather.6
  1886.3 117.0 reduce-scatter.10
  2007.3 117.0 reduce-scatter.8
  2128.6 414.7 reduce-scatter.4
  2547.4 414.7 reduce-scatter.6
where the time goes:
time: 2980 us; the launch traced here: 2970 us
  waiting for transfers between devices  1540 us (52%)
  matrix products  1310 us (44%)
  local copies, waits for them, and re-layouts  80.4 us (3%)
    reduce_scatter x4, waiting for transfers between devices, device_body(): lax.psum_scatter(grad_stack, 'stage', scatter_dimension=0, tiled=True)  1070 us
    all_gather x4, waiting for transfers between devices, gather_round(): lax.all_gather(weight[round_idx], 'stage')  462 us
    dot_general x16, matrix products, layer_forward(): resid_delta = jnp.dot(gelu_out, w_down, preferred_element_type=jnp.float32)  323 us
    dot_general x16, matrix products, layer_backward(): jnp.einsum('td,fd->tf', grad_next, w_down, preferred_element_type=jnp.flo...  276 us
    dot_general x16, matrix products, layer_backward(): jnp.einsum('tf,td->fd', gelu_out, grad_next, preferred_element_type=jnp.f...  208 us
    dot_general x16, matrix products, layer_backward(): pre_act = jnp.dot(hidden, w_up, preferred_element_type=jnp.float32)  180 us
    dot_general x16, matrix products, layer_backward(): jnp.einsum('td,tf->df', hidden, d_pre, preferred_element_type=jnp.float32)  177 us
    dot_general x16, matrix products, layer_backward(): jnp.einsum('tf,df->td', d_pre, w_up, preferred_element_type=jnp.float32)  149 us
  transfers between devices with their start and end apart: 8, of which 8 were waited for; matrix products, arithmetic and copies ran while one was open for 0% of the time, Pallas kernels for 0%

commit v1 on v0

v1 whole, which is shorter than its diff:
```python
import functools

import jax
import jax.numpy as jnp
from jax import lax
from jax.experimental import pallas as pl
from jax.experimental.pallas import tpu as pltpu
from jax.sharding import PartitionSpec as P

MESH = pl.DeviceIdType.MESH
ANY = pl.BlockSpec(memory_space=pl.ANY)
VMEM_LIMIT = 67043328

GELU_C = 0.7978845608028654
GELU_K = 0.044715

ROWS = 256
HOP = 2
SLOTS = 4
WIDE_COLS = 512
F_ORDER = 'zzzczczczcccyo'
B_ORDER = 'dmxxpxpxpxpxpp'
FB_ORDER = 'zdzmzczcxzcxzcccpxpxpyxpxpop'

NT = (((1,), (1,)), ((), ()))
TN = (((0,), (0,)), ((), ()))


def mm(lhs, rhs, dims=(((1,), (0,)), ((), ()))):
    return lax.dot_general(lhs, rhs, dims, preferred_element_type=jnp.float32)


def gelu_and_slope(z):
    zz = z * z
    half = 0.5 + 0.5 * jnp.tanh(z * (GELU_C + (GELU_C * GELU_K) * zz))
    act = z * half
    return act, half + act * (1.0 - half) * (2.0 * GELU_C + (6.0 * GELU_C * GELU_K) * zz)


def blocks(size, width):
    return [slice(start, min(start + width, size)) for start in range(0, size, width)]


def forward_tasks(h, weights, saved, done):
    ua, wa, ub, wb = weights
    a_buf, gp_buf, mid_buf, ab_buf, gpb_buf = saved
    cols = blocks(ua.shape[1], WIDE_COLS)

    def wide_up():
        for part in cols:
            act, slope = gelu_and_slope(mm(h[...], ua[:, part]))
            a_buf[:, part] = act.astype(jnp.bfloat16)
            gp_buf[:, part] = slope
            yield

    def wide_down():
        total = 0.0
        for k, part in enumerate(cols):
            product = mm(a_buf[:, part], wa[part, :])
            total = product if k == 0 else total + product
            if k == len(cols) - 1:
                mid_buf[...] = (h[...].astype(jnp.float32) + total).astype(jnp.bfloat16)
            yield

    def narrow_up():
        act, slope = gelu_and_slope(mm(mid_buf[...], ub[...]))
        ab_buf[...] = act.astype(jnp.bfloat16)
        gpb_buf[...] = slope
        yield

    def narrow_down():
        done((mid_buf[...].astype(jnp.float32) + mm(ab_buf[...], wb[...])).astype(jnp.bfloat16))
        yield

    return dict(z=wide_up(), c=wide_down(), y=narrow_up(), o=narrow_down())


def backward_tasks(g, weights, slopes, kept, done):
    ua, wa, ub, wb = weights
    gp_buf, gpb_buf = slopes
    dzb_buf, gmid_buf, dz_buf = kept
    cols = blocks(wa.shape[0], WIDE_COLS)

    def narrow_down():
        dzb_buf[...] = (mm(g[...], wb[...], NT) * gpb_buf[...]).astype(jnp.bfloat16)
        yield

    def narrow_up():
        gmid_buf[...] = (g[...].astype(jnp.float32) + mm(dzb_buf[...], ub[...], NT)).astype(jnp.bfloat16)
        yield

    def wide_down():
        for part in cols:
            dz_buf[:, part] = (mm(gmid_buf[...], wa[part, :], NT) * gp_buf[:, part]).astype(jnp.bfloat16)
            yield

    def wide_up():
        total = 0.0
        for k, part in enumerate(cols):
            product = mm(dz_buf[:, part], ua[:, part], NT)
            total = product if k == 0 else total + product
            if k == len(cols) - 1:
                done((gmid_buf[...].astype(jnp.float32) + total).astype(jnp.bfloat16))
            yield

    return dict(d=narrow_down(), m=narrow_up(), x=wide_down(), p=wide_up())


def run_tasks(order, tasks):
    for name in order:
        next(tasks[name])


def add_product(total, lhs, rhs, width):
    for rows in blocks(total.shape[0], width):
        total[rows, :] += mm(lhs[:, rows].T, rhs[...])


def kernel(
    axis, acts, gout, ua_hbm, wa_hbm, ub_hbm, wb_hbm,
    acts_out, grad_in, dua_hbm, dwa_hbm, dub_hbm, dwb_hbm,
    h_all, g_all, mid_all, a_all, gp_all, ab_all, gpb_all,
    ua, wa, ub, wb, dua, dwa, dub, dwb,
    h_buf, a_buf, gp_buf, mid_buf, ab_buf, gpb_buf, f_send,
    g_buf, gp_in, gpb_in, dzb_buf, gmid_buf, dz_buf, b_send,
    a_in, h_in, mid_in, ab_in,
    got_h, got_g, got_out, got_gin, f_sem, b_sem, feed_h_sem, feed_g_sem,
    h_sem, g_sem, gp_sem, gpb_sem, w_sem, st_sem, param_sem,
):
    me = lax.axis_index(axis)
    stages = lax.axis_size(axis)
    last = stages - 1
    own = acts.shape[0]
    chunks = own * stages
    span = HOP * last

    weights = (ua, wa, ub, wb)

    def fwd_chunk(t):
        return t - HOP * me

    def bwd_chunk(t):
        return t - 2 * span - 1 + HOP * me

    def valid(c):
        return (c >= 0) & (c < chunks)

    def on(device):
        return dict(device_id={axis: device}, device_id_type=MESH)

    def load(src, dst, sem):
        return pltpu.make_async_copy(src, dst, sem)

    params = [load(src, dst, param_sem.at[k]) for k, (src, dst) in enumerate(
        [(ua_hbm, ua), (wa_hbm, wa), (ub_hbm, ub), (wb_hbm, wb)])]
    for copy in params:
        copy.start()

    def arrival(buf, c, sem):
        return pltpu.make_async_remote_copy(buf.at[c], buf.at[c], sem.at[c], sem.at[c], **on(me))

    def fetch_h(c):
        @pl.when(valid(c))
        def _():
            local = (me == 0) & (c < own)

            @pl.when(local)
            def _():
                load(acts.at[lax.rem(c, own)], h_buf, h_sem).start()

            @pl.when(jnp.logical_not(local))
            def _():
                arrival(h_all, c, got_h).wait_recv()
                load(h_all.at[c], h_buf, h_sem).start()

    def fetch_g(c):
        @pl.when(valid(c))
        def _():
            load(gp_all.at[c], gp_in, gp_sem).start()
            load(gpb_all.at[c], gpb_in, gpb_sem).start()
            local = (me == last) & (c >= chunks - own)
            buf = g_buf.at[lax.rem(c, 2)]

            @pl.when(local)
            def _():
                load(gout.at[lax.rem(c, own)], buf, g_sem).start()

            @pl.when(jnp.logical_not(local))
            def _():
                arrival(g_all, c, got_g).wait_recv()
                load(g_all.at[c], buf, g_sem).start()

    def fetch_weight_operands(c):
        local_h = (me == 0) & (c < own)

        @pl.when(local_h)
        def _():
            load(acts.at[lax.rem(c, own)], h_in, w_sem.at[0]).start()

        @pl.when(jnp.logical_not(local_h))
        def _():
            load(h_all.at[c], h_in, w_sem.at[0]).start()
        load(a_all.at[c], a_in, w_sem.at[1]).start()
        load(mid_all.at[c], mid_in, w_sem.at[2]).start()
        load(ab_all.at[c], ab_in, w_sem.at[3]).start()

    def send(slot_ref, sem, c, inner, next_device, next_all, next_sem, home_out, home_sem):
        home = c // own
        spot = lax.rem(c, own)

        @pl.when(inner)
        def _():
            pltpu.make_async_remote_copy(slot_ref, next_all.at[c], sem, next_sem.at[c], **on(next_device)).start()

        @pl.when(jnp.logical_not(inner) & (home != me))
        def _():
            pltpu.make_async_remote_copy(slot_ref, home_out.at[spot], sem, home_sem.at[spot], **on(home)).start()

        @pl.when(jnp.logical_not(inner) & (home == me))
        def _():
            load(slot_ref, home_out.at[spot], sem).start()

    def sent(slot_ref, sem):
        load(slot_ref, slot_ref, sem).wait()

    def store_copies(c):
        pairs = [(a_buf, a_all), (gp_buf, gp_all), (mid_buf, mid_all), (ab_buf, ab_all), (gpb_buf, gpb_all)]
        return [load(src, dst.at[c], st_sem.at[k]) for k, (src, dst) in enumerate(pairs)]

    fetch_h(fwd_chunk(0))
    for total in (dua, dwa, dub, dwb):
        total[...] = jnp.zeros_like(total)
    for copy in params:
        copy.wait()

    def step(t, _):
        cf, cb = fwd_chunk(t), bwd_chunk(t)
        has_f, has_b = valid(cf), valid(cb)
        fed = t + own - own * me

        @pl.when((me != 0) & (fed >= 0) & (fed < own))
        def _():
            pltpu.make_async_remote_copy(acts.at[fed], h_all.at[own * me + fed], feed_h_sem.at[fed], got_h.at[own * me + fed], **on(0)).start()

        fed_g = t - own * me

        @pl.when((me != last) & (fed_g >= 0) & (fed_g < own))
        def _():
            pltpu.make_async_remote_copy(gout.at[fed_g], g_all.at[own * me + fed_g], feed_g_sem.at[fed_g], got_g.at[own * me + fed_g], **on(last)).start()

        @pl.when(has_b)
        def _():
            fetch_weight_operands(cb)

        g_now = g_buf.at[lax.rem(jnp.maximum(cb, 0), 2)]
        f_slot, b_slot = lax.rem(cf, SLOTS), lax.rem(cb, SLOTS)

        def f_begin():
            load(h_buf, h_buf, h_sem).wait()

            @pl.when(cf >= SLOTS)
            def _():
                sent(f_send.at[f_slot], f_sem.at[f_slot])

        def f_tasks():
            def done(h):
                f_send[f_slot] = h
            return forward_tasks(h_buf, weights, (a_buf, gp_buf, mid_buf, ab_buf, gpb_buf), done)

        def f_end():
            send(f_send.at[f_slot], f_sem.at[f_slot], cf, me != last, me + 1, h_all, got_h, acts_out, got_out)
            for copy in store_copies(cf):
                copy.start()

        def b_begin():
            load(g_buf.at[0], g_buf.at[0], g_sem).wait()
            load(gp_in, gp_in, gp_sem).wait()
            load(gpb_in, gpb_in, gpb_sem).wait()

            @pl.when(cb >= SLOTS)
            def _():
                sent(b_send.at[b_slot], b_sem.at[b_slot])

        def b_tasks():
            def done(g):
                b_send[b_slot] = g
            return backward_tasks(g_now, weights, (gp_in, gpb_in), (dzb_buf, gmid_buf, dz_buf), done)

        def b_end():
            send(b_send.at[b_slot], b_sem.at[b_slot], cb, me != 0, me - 1, g_all, got_g, grad_in, got_gin)

        @pl.when(has_f & has_b)
        def _():
            f_begin()
            b_begin()
            run_tasks(FB_ORDER, f_tasks() | b_tasks())
            b_end()
            f_end()

        @pl.when(has_f & jnp.logical_not(has_b))
        def _():
            f_begin()
            run_tasks(F_ORDER, f_tasks())
            f_end()

        @pl.when(has_b & jnp.logical_not(has_f))
        def _():
            b_begin()
            run_tasks(B_ORDER, b_tasks())
            b_end()

        @pl.when(has_f)
        def _():
            for copy in store_copies(cf):
                copy.wait()

        fetch_g(cb + 1)
        fetch_h(cf + 1)

        @pl.when(has_b)
        def _():
            for k, buf in enumerate((h_in, a_in, mid_in, ab_in)):
                load(buf, buf, w_sem.at[k]).wait()
            add_product(dwb, ab_in, g_now, 256)
            add_product(dub, mid_in, dzb_buf, 256)
            add_product(dwa, a_in, gmid_buf, 256)
            add_product(dua, h_in, dz_buf, 256)
        return 0

    lax.fori_loop(0, chunks + 2 * span + 1, step, 0)

    finals = [load(src, dst, param_sem.at[k]) for k, (src, dst) in enumerate(
        [(dua, dua_hbm), (dwa, dwa_hbm), (dub, dub_hbm), (dwb, dwb_hbm)])]
    for copy in finals:
        copy.start()
    for slot in range(SLOTS):
        sent(f_send.at[slot], f_sem.at[slot])
        sent(b_send.at[slot], b_sem.at[slot])

    def settle(k, _):
        @pl.when(me != 0)
        def _():
            load(acts.at[k], acts.at[k], feed_h_sem.at[k]).wait()
            arrival(grad_in, k, got_gin).wait_recv()

        @pl.when(me != last)
        def _():
            load(gout.at[k], gout.at[k], feed_g_sem.at[k]).wait()
            arrival(acts_out, k, got_out).wait_recv()
        return 0

    lax.fori_loop(0, own, settle, 0)
    for copy in finals:
        copy.wait()


def run_stages(axis, stages, acts, gout, ua, wa, ub, wb):
    tokens, width = acts.shape
    own = tokens // ROWS
    chunks = own * stages
    wide, narrow = ua.shape[1], ub.shape[1]
    bf, f32 = jnp.bfloat16, jnp.float32
    shape = jax.ShapeDtypeStruct
    outs = [
        shape((own, ROWS, width), bf), shape((own, ROWS, width), bf),
        shape(ua.shape, f32), shape(wa.shape, f32), shape(ub.shape, f32), shape(wb.shape, f32),
        shape((chunks, ROWS, width), bf), shape((chunks, ROWS, width), bf), shape((chunks, ROWS, width), bf),
        shape((chunks, ROWS, wide), bf), shape((chunks, ROWS, wide), f32),
        shape((chunks, ROWS, narrow), bf), shape((chunks, ROWS, narrow), f32),
    ]
    vm, dma = pltpu.VMEM, pltpu.SemaphoreType.DMA
    tok, wid, nar = (ROWS, width), (ROWS, wide), (ROWS, narrow)
    scratch = [
        vm(ua.shape, bf), vm(wa.shape, bf), vm(ub.shape, bf), vm(wb.shape, bf),
        vm(ua.shape, f32), vm(wa.shape, f32), vm(ub.shape, f32), vm(wb.shape, f32),
        vm(tok, bf), vm(wid, bf), vm(wid, f32), vm(tok, bf), vm(nar, bf), vm(nar, f32), vm((SLOTS,) + tok, bf),
        vm((2,) + tok, bf), vm(wid, f32), vm(nar, f32), vm(nar, bf), vm(tok, bf), vm(wid, bf), vm((SLOTS,) + tok, bf),
        vm(wid, bf), vm(tok, bf), vm(tok, bf), vm(nar, bf),
        dma((chunks,)), dma((chunks,)), dma((own,)), dma((own,)), dma((SLOTS,)), dma((SLOTS,)), dma((own,)), dma((own,)),
        dma, dma, dma, dma, dma((4,)), dma((5,)), dma((4,)),
    ]
    results = pl.pallas_call(
        functools.partial(kernel, axis),
        out_shape=outs,
        in_specs=[ANY] * 6,
        out_specs=[ANY] * len(outs),
        scratch_shapes=scratch,
        compiler_params=pltpu.CompilerParams(vmem_limit_bytes=VMEM_LIMIT, has_side_effects=True),
    )(acts.reshape(own, ROWS, width), gout.reshape(own, ROWS, width), ua, wa, ub, wb)
    return results[:6]


def solution(mesh):
    tok_spec = P(('data', 'stage'))
    row_spec = P('stage')
    stages = mesh.shape['stage']

    def device_body(acts_in, grad_out, w_up_a, w_down_a, w_up_b, w_down_b):
        tokens, width = acts_in.shape[0] * acts_in.shape[1], acts_in.shape[2]
        out, gin, dua, dwa, dub, dwb = run_stages(
            'stage', stages, acts_in.reshape(tokens, width), grad_out.reshape(tokens, width),
            w_up_a[0], w_down_a[0], w_up_b[0], w_down_b[0])
        return (out.reshape(acts_in.shape), gin.reshape(acts_in.shape), dua[None], dwa[None], dub[None], dwb[None])

    return jax.shard_map(device_body, mesh=mesh, in_specs=(tok_spec, tok_spec, row_spec, row_spec, row_spec, row_spec), out_specs=(tok_spec,) * 6, check_vma=False)
```

time: 2980 us -> 1010 us (0.34)
  waiting for transfers between devices: 1540 us -> 0 us
  matrix products: 1310 us -> 0 us
  Pallas kernels: 0 us -> 991 us
  local copies, waits for them, and re-layouts: 80.4 us -> 21.9 us
    dot_general x96 -> x0, matrix products: 1310 us -> none  [the longest x16 323 us: layer_forward(): resid_delta = jnp.dot(gelu_out, w_down, preferred_element_type=jnp.float32)]
    reduce_scatter x4 -> x0, waiting for transfers between devices: 1070 us -> none  [device_body(): lax.psum_scatter(grad_stack, 'stage', scatter_dimension=0, tiled=True)]
    pallas_call x0 -> x1, Pallas kernels: none -> 991 us  [run_stages(): pl.pallas_call(functools.partial(kernel, axis), out_shape=outs, in_specs=...]
    all_gather x4 -> x0, waiting for transfers between devices: 462 us -> none  [gather_round(): lax.all_gather(weight[round_idx], 'stage')]
    broadcast_in_dim x2 -> x0, local copies, waits for them, and re-layouts: 47.8 us -> none  [device_body(): lax.scan(pair_backward, grad_h, (saved_acts[round_idx], round_weights), r...]
  transfers between devices with their start and end apart: 8 -> 0, of which waited for: 8 -> 0; matrix products, arithmetic and copies ran while one was open for 0% -> 0% of each run, Pallas kernels for 0% -> 0%
where the time goes in v1:
time: 1010 us
  Pallas kernels  991 us (98%)
  local copies, waits for them, and re-layouts  21.9 us (2%)
    pallas_call x1, Pallas kernels, run_stages(): pl.pallas_call(functools.partial(kernel, axis), out_shape=outs, in_specs=...  991 us
    unnamed x20, local copies, waits for them, and re-layouts  21.9 us

profile of v1, /device:TPU:0, one launch (start us, length us, event | category | flops | bytes accessed | tf_op | source)
XLA Modules:
  0.0 1013.1 jit_solution(14862515412070452930)
XLA Ops:
  0.6 990.6 %shard_map.109 = (bf16[8,256,768]{2,1,0:T(8,128)(2,1)}, bf16[8,256,768]{2,1,0:T(8,128)(2,1)}, f32[768,3072]{1,0:T(8,128)}, f32[3072,768]{1,0:T(8,128)}, f32[768,...) custom-call(bf16[8,256,768]{2,1,0:T(8,128)(2,1)} %bitcast.20, ...), custom_call_target="tpu_custom_call" | custom-call | tf_op jit(solution)/shard_map/pallas_call | solution.py:382
  991.2 0.0 copy-start.1
  991.2 0.0 copy-start
  991.2 3.9 copy.18
  995.1 0.0 copy-done.1
  995.1 0.0 slice-start
  995.1 1.7 copy.19
  996.8 2.3 copy-done
  999.1 0.0 slice-start.1
  999.1 0.0 slice-start.2
  999.1 4.8 copy.20
  1003.9 0.0 slice-done
  1003.9 1.2 slice-done.1
  1005.0 0.2 slice-done.2
  1005.3 0.0 copy-start.3
  1005.3 4.0 copy.21
  1009.2 0.0 copy-done.3
  1009.2 0.0 copy-start.2
  1009.2 1.4 copy.22
  1010.6 1.1 copy-done.2
  1011.7 1.4 copy.23
  (1 shorter events, 0.0 us)
Async XLA Ops:
  991.2 3.9 copy-start.1
  991.2 7.8 copy-start
  995.1 8.7 slice-start
  999.1 6.0 slice-start.1
  999.1 6.2 slice-start.2
  1005.3 4.0 copy-start.3
  1009.2 2.5 copy-start.2

commit v2 on v1

--- a/solution.py
+++ b/solution.py
@@ -15,12 +15,12 @@
 GELU_K = 0.044715
 
 ROWS = 256
-HOP = 2
+HOP = 3
 SLOTS = 4
 WIDE_COLS = 512
-F_ORDER = 'zzzczczczcccyo'
+F_ORDER = 'zzczczczczccyo'
 B_ORDER = 'dmxxpxpxpxpxpp'
-FB_ORDER = 'zdzmzczcxzcxzcccpxpxpyxpxpop'
+FB_ORDER = 'zdmzxzcxpzcxpzcxpzccpxcxpypo'
 
 NT = (((1,), (1,)), ((), ()))
 TN = (((0,), (0,)), ((), ()))
@@ -314,8 +314,12 @@
             for copy in store_copies(cf):
                 copy.wait()
 
-        fetch_g(cb + 1)
-        fetch_h(cf + 1)
+        steady = valid(cf + 1)
+
+        @pl.when(steady)
+        def _():
+            fetch_g(cb + 1)
+            fetch_h(cf + 1)
 
         @pl.when(has_b)
         def _():
@@ -325,6 +329,10 @@
             add_product(dub, mid_in, dzb_buf, 256)
             add_product(dwa, a_in, gmid_buf, 256)
             add_product(dua, h_in, dz_buf, 256)
+
+        @pl.when(jnp.logical_not(steady))
+        def _():
+            fetch_g(cb + 1)
         return 0
 
     lax.fori_loop(0, chunks + 2 * span + 1, step, 0)

time: 1010 us -> 1050 us (1.040)
  Pallas kernels: 991 us -> 1020 us
    pallas_call x1, Pallas kernels: 991 us -> 1020 us  [run_stages(): pl.pallas_call(functools.partial(kernel, axis), out_shape=outs, in_specs=...]
where the time goes in v2:
time: 1050 us
  Pallas kernels  1020 us (97%)
  local copies, waits for them, and re-layouts  21.9 us (2%)
    pallas_call x1, Pallas kernels, run_stages(): pl.pallas_call(functools.partial(kernel, axis), out_shape=outs, in_specs=...  1020 us
    unnamed x20, local copies, waits for them, and re-layouts  21.9 us

profile of v2, /device:TPU:0, one launch (start us, length us, event | category | flops | bytes accessed | tf_op | source)
XLA Modules:
  0.0 1046.6 jit_solution(1925822708224884862)
XLA Ops:
  0.6 1024.0 %shard_map.109 = (bf16[8,256,768]{2,1,0:T(8,128)(2,1)}, bf16[8,256,768]{2,1,0:T(8,128)(2,1)}, f32[768,3072]{1,0:T(8,128)}, f32[3072,768]{1,0:T(8,128)}, f32[768,...) custom-call(bf16[8,256,768]{2,1,0:T(8,128)(2,1)} %bitcast.20, ...), custom_call_target="tpu_custom_call" | custom-call | tf_op jit(solution)/shard_map/pallas_call | solution.py:390
  1024.7 0.0 copy-start.1
  1024.7 0.0 copy-start
  1024.7 3.9 copy.18
  1028.6 0.0 copy-done.1
  1028.6 0.0 slice-start
  1028.6 1.7 copy.19
  1030.3 2.3 copy-done
  1032.5 0.0 slice-start.1
  1032.5 0.0 slice-start.2
  1032.6 4.8 copy.20
  1037.3 0.0 slice-done
  1037.3 1.2 slice-done.1
  1038.5 0.2 slice-done.2
  1038.7 0.0 copy-start.3
  1038.7 4.0 copy.21
  1042.7 0.0 copy-done.3
  1042.7 0.0 copy-start.2
  1042.7 1.4 copy.22
  1044.1 1.1 copy-done.2
  1045.2 1.4 copy.23
  (1 shorter events, 0.0 us)
Async XLA Ops:
  1024.7 3.9 copy-start.1
  1024.7 7.8 copy-start
  1028.6 8.7 slice-start
  1032.5 6.0 slice-start.1
  1032.5 6.2 slice-start.2
  1038.7 4.0 copy-start.3
  1042.7 2.5 copy-start.2

commit v3 on v2

--- a/solution.py
+++ b/solution.py
@@ -15,7 +15,8 @@
 GELU_K = 0.044715
 
 ROWS = 256
-HOP = 3
+HOP = 2
+LAG = 2
 SLOTS = 4
 WIDE_COLS = 512
 F_ORDER = 'zzczczczczccyo'
@@ -132,15 +133,19 @@
     last = stages - 1
     own = acts.shape[0]
     chunks = own * stages
-    span = HOP * last
+
+    def offset(stage):
+        return HOP * stage + stage // (stages // 2)
+
+    span = offset(last)
 
     weights = (ua, wa, ub, wb)
 
     def fwd_chunk(t):
-        return t - HOP * me
+        return t - offset(me)
 
     def bwd_chunk(t):
-        return t - 2 * span - 1 + HOP * me
+        return t - 2 * span - LAG + offset(me)
 
     def valid(c):
         return (c >= 0) & (c < chunks)
@@ -173,11 +178,16 @@
                 arrival(h_all, c, got_h).wait_recv()
                 load(h_all.at[c], h_buf, h_sem).start()
 
+    def fetch_slopes(c):
+        @pl.when(valid(c))
+        def _():
+            side = lax.rem(c, 2)
+            load(gp_all.at[c], gp_in.at[side], gp_sem.at[side]).start()
+            load(gpb_all.at[c], gpb_in.at[side], gpb_sem.at[side]).start()
+
     def fetch_g(c):
         @pl.when(valid(c))
         def _():
-            load(gp_all.at[c], gp_in, gp_sem).start()
-            load(gpb_all.at[c], gpb_in, gpb_sem).start()
             local = (me == last) & (c >= chunks - own)
             buf = g_buf.at[lax.rem(c, 2)]
 
@@ -248,11 +258,19 @@
         def _():
             pltpu.make_async_remote_copy(gout.at[fed_g], g_all.at[own * me + fed_g], feed_g_sem.at[fed_g], got_g.at[own * me + fed_g], **on(last)).start()
 
+        @pl.when(valid(cf - 1))
+        def _():
+            for copy in store_copies(cf - 1):
+                copy.wait()
+
+        fetch_slopes(cb + 1)
+
         @pl.when(has_b)
         def _():
             fetch_weight_operands(cb)
 
-        g_now = g_buf.at[lax.rem(jnp.maximum(cb, 0), 2)]
+        b_side = lax.rem(jnp.maximum(cb, 0), 2)
+        g_now, gp_now, gpb_now = g_buf.at[b_side], gp_in.at[b_side], gpb_in.at[b_side]
         f_slot, b_slot = lax.rem(cf, SLOTS), lax.rem(cb, SLOTS)
 
         def f_begin():
@@ -274,8 +292,8 @@
 
         def b_begin():
             load(g_buf.at[0], g_buf.at[0], g_sem).wait()
-            load(gp_in, gp_in, gp_sem).wait()
-            load(gpb_in, gpb_in, gpb_sem).wait()
+            load(gp_now, gp_now, gp_sem.at[b_side]).wait()
+            load(gpb_now, gpb_now, gpb_sem.at[b_side]).wait()
 
             @pl.when(cb >= SLOTS)
             def _():
@@ -284,7 +302,7 @@
         def b_tasks():
             def done(g):
                 b_send[b_slot] = g
-            return backward_tasks(g_now, weights, (gp_in, gpb_in), (dzb_buf, gmid_buf, dz_buf), done)
+            return backward_tasks(g_now, weights, (gp_now, gpb_now), (dzb_buf, gmid_buf, dz_buf), done)
 
         def b_end():
             send(b_send.at[b_slot], b_sem.at[b_slot], cb, me != 0, me - 1, g_all, got_g, grad_in, got_gin)
@@ -308,11 +326,6 @@
             b_begin()
             run_tasks(B_ORDER, b_tasks())
             b_end()
-
-        @pl.when(has_f)
-        def _():
-            for copy in store_copies(cf):
-                copy.wait()
 
         steady = valid(cf + 1)
 
@@ -335,7 +348,7 @@
             fetch_g(cb + 1)
         return 0
 
-    lax.fori_loop(0, chunks + 2 * span + 1, step, 0)
+    lax.fori_loop(0, chunks + 2 * span + LAG, step, 0)
 
     finals = [load(src, dst, param_sem.at[k]) for k, (src, dst) in enumerate(
         [(dua, dua_hbm), (dwa, dwa_hbm), (dub, dub_hbm), (dwb, dwb_hbm)])]
@@ -382,10 +395,10 @@
         vm(ua.shape, bf), vm(wa.shape, bf), vm(ub.shape, bf), vm(wb.shape, bf),
         vm(ua.shape, f32), vm(wa.shape, f32), vm(ub.shape, f32), vm(wb.shape, f32),
         vm(tok, bf), vm(wid, bf), vm(wid, f32), vm(tok, bf), vm(nar, bf), vm(nar, f32), vm((SLOTS,) + tok, bf),
-        vm((2,) + tok, bf), vm(wid, f32), vm(nar, f32), vm(nar, bf), vm(tok, bf), vm(wid, bf), vm((SLOTS,) + tok, bf),
+        vm((2,) + tok, bf), vm((2,) + wid, f32), vm((2,) + nar, f32), vm(nar, bf), vm(tok, bf), vm(wid, bf), vm((SLOTS,) + tok, bf),
         vm(wid, bf), vm(tok, bf), vm(tok, bf), vm(nar, bf),
         dma((chunks,)), dma((chunks,)), dma((own,)), dma((own,)), dma((SLOTS,)), dma((SLOTS,)), dma((own,)), dma((own,)),
-        dma, dma, dma, dma, dma((4,)), dma((5,)), dma((4,)),
+        dma, dma, dma((2,)), dma((2,)), dma((4,)), dma((5,)), dma((4,)),
     ]
     results = pl.pallas_call(
         functools.partial(kernel, axis),

time: 1050 us -> 908 us (0.86)
  Pallas kernels: 1020 us -> 884 us
    pallas_call x1, Pallas kernels: 1020 us -> 884 us  [run_stages(): pl.pallas_call(functools.partial(kernel, axis), out_shape=outs, in_specs=...]
where the time goes in v3:
time: 908 us; the launch traced here: 907 us
  Pallas kernels  884 us (97%)
  local copies, waits for them, and re-layouts  21.9 us (2%)
    pallas_call x1, Pallas kernels, run_stages(): pl.pallas_call(functools.partial(kernel, axis), out_shape=outs, in_specs=...  884 us
    unnamed x20, local copies, waits for them, and re-layouts  21.9 us

profile of v3, /device:TPU:0, one launch (start us, length us, event | category | flops | bytes accessed | tf_op | source)
XLA Modules:
  0.0 907.0 jit_solution(18311418955904387637)
XLA Ops:
  0.6 884.4 %shard_map.109 = (bf16[8,256,768]{2,1,0:T(8,128)(2,1)}, bf16[8,256,768]{2,1,0:T(8,128)(2,1)}, f32[768,3072]{1,0:T(8,128)}, f32[3072,768]{1,0:T(8,128)}, f32[768,...) custom-call(bf16[8,256,768]{2,1,0:T(8,128)(2,1)} %bitcast.20, ...), custom_call_target="tpu_custom_call" | custom-call | tf_op jit(solution)/shard_map/pallas_call | solution.py:403
  885.1 0.0 copy-start.1
  885.1 0.0 copy-start
  885.1 3.9 copy.18
  889.0 0.0 copy-done.1
  889.0 0.0 slice-start
  889.0 1.7 copy.19
  890.6 2.3 copy-done
  892.9 0.0 slice-start.1
  892.9 0.0 slice-start.2
  892.9 4.8 copy.20
  897.7 0.0 slice-done
  897.7 1.2 slice-done.1
  898.9 0.2 slice-done.2
  899.1 0.0 copy-start.3
  899.1 4.0 copy.21
  903.1 0.0 copy-done.3
  903.1 0.0 copy-start.2
  903.1 1.4 copy.22
  904.5 1.1 copy-done.2
  905.6 1.4 copy.23
  (1 shorter events, 0.0 us)
Async XLA Ops:
  885.1 3.9 copy-start.1
  885.1 7.8 copy-start
  889.0 8.7 slice-start
  892.9 6.0 slice-start.1
  892.9 6.2 slice-start.2
  899.1 4.0 copy-start.3
  903.1 2.5 copy-start.2

commit v4 on v3

--- a/solution.py
+++ b/solution.py
@@ -135,7 +135,7 @@
     chunks = own * stages
 
     def offset(stage):
-        return HOP * stage + stage // (stages // 2)
+        return HOP * stage + stage // 2
 
     span = offset(last)
 

time: 908 us -> 910 us (level)
  no operation moved by 1% of the time
where the time goes in v4:
time: 910 us; the launch traced here: 909 us
  Pallas kernels  886 us (97%)
  local copies, waits for them, and re-layouts  21.9 us (2%)
    pallas_call x1, Pallas kernels, run_stages(): pl.pallas_call(functools.partial(kernel, axis), out_shape=outs, in_specs=...  886 us
    unnamed x20, local copies, waits for them, and re-layouts  21.9 us

profile of v4, /device:TPU:0, one launch (start us, length us, event | category | flops | bytes accessed | tf_op | source)
XLA Modules:
  0.0 908.7 jit_solution(13909029568443449105)
XLA Ops:
  0.6 886.1 %shard_map.109 = (bf16[8,256,768]{2,1,0:T(8,128)(2,1)}, bf16[8,256,768]{2,1,0:T(8,128)(2,1)}, f32[768,3072]{1,0:T(8,128)}, f32[3072,768]{1,0:T(8,128)}, f32[768,...) custom-call(bf16[8,256,768]{2,1,0:T(8,128)(2,1)} %bitcast.20, ...), custom_call_target="tpu_custom_call" | custom-call | tf_op jit(solution)/shard_map/pallas_call | solution.py:403
  886.7 0.0 copy-start.1
  886.7 0.0 copy-start
  886.7 3.9 copy.18
  890.6 0.0 copy-done.1
  890.6 0.0 slice-start
  890.6 1.7 copy.19
  892.3 2.3 copy-done
  894.6 0.0 slice-start.1
  894.6 0.0 slice-start.2
  894.6 4.8 copy.20
  899.4 0.0 slice-done
  899.4 1.2 slice-done.1
  900.5 0.2 slice-done.2
  900.8 0.0 copy-start.3
  900.8 4.0 copy.21
  904.7 0.0 copy-done.3
  904.7 0.0 copy-start.2
  904.7 1.4 copy.22
  906.1 1.1 copy-done.2
  907.3 1.4 copy.23
  (1 shorter events, 0.0 us)
Async XLA Ops:
  886.7 3.9 copy-start.1
  886.7 7.8 copy-start
  890.6 8.7 slice-start
  894.6 6.0 slice-start.1
  894.6 6.2 slice-start.2
  900.8 4.0 copy-start.3
  904.7 2.5 copy-start.2

commit v5 on v4

--- a/solution.py
+++ b/solution.py
@@ -120,12 +120,12 @@
 def kernel(
     axis, acts, gout, ua_hbm, wa_hbm, ub_hbm, wb_hbm,
     acts_out, grad_in, dua_hbm, dwa_hbm, dub_hbm, dwb_hbm,
-    h_all, g_all, mid_all, a_all, gp_all, ab_all, gpb_all,
+    h_all, g_all, relay, mid_all, a_all, gp_all, ab_all, gpb_all,
     ua, wa, ub, wb, dua, dwa, dub, dwb,
     h_buf, a_buf, gp_buf, mid_buf, ab_buf, gpb_buf, f_send,
     g_buf, gp_in, gpb_in, dzb_buf, gmid_buf, dz_buf, b_send,
     a_in, h_in, mid_in, ab_in,
-    got_h, got_g, got_out, got_gin, f_sem, b_sem, feed_h_sem, feed_g_sem,
+    got_h, got_g, got_out, got_gin, f_sem, b_sem, feed_h_sem, feed_g_sem, got_relay, relay_sem,
     h_sem, g_sem, gp_sem, gpb_sem, w_sem, st_sem, param_sem,
 ):
     me = lax.axis_index(axis)
@@ -233,6 +233,52 @@
     def sent(slot_ref, sem):
         load(slot_ref, slot_ref, sem).wait()
 
+    half = stages // 2
+    first_half, edge = me < half, half // 2
+
+    def feed_acts(t):
+        by_way = (me >= edge) & first_half
+        lead = jnp.where(me == 1, own, jnp.where(by_way, 2 * own, own + own // 2))
+        spot = t + lead - own * me
+        due = (me != 0) & (spot >= 0) & (spot < own)
+
+        @pl.when(due & jnp.logical_not(by_way))
+        def _():
+            pltpu.make_async_remote_copy(acts.at[spot], h_all.at[own * me + spot], feed_h_sem.at[spot], got_h.at[own * me + spot], **on(0)).start()
+
+        @pl.when(due & by_way)
+        def _():
+            pltpu.make_async_remote_copy(acts.at[spot], relay.at[spot], feed_h_sem.at[spot], got_relay.at[spot], **on(me + half)).start()
+
+        spot = t + own + own // 4 - own * (me - half)
+
+        @pl.when((me >= half + edge) & (spot >= 0) & (spot < own))
+        def _():
+            arrival(relay, spot, got_relay).wait_recv()
+            c = own * (me - half) + spot
+            pltpu.make_async_remote_copy(relay.at[spot], h_all.at[c], relay_sem.at[spot], got_h.at[c], **on(0)).start()
+
+    def feed_grads(t):
+        by_way = jnp.logical_not(first_half) & (me < half + edge)
+        spot = t - own // 2 - own * me
+        due = (me != last) & (spot >= 0) & (spot < own)
+
+        @pl.when(due & jnp.logical_not(by_way))
+        def _():
+            pltpu.make_async_remote_copy(gout.at[spot], g_all.at[own * me + spot], feed_g_sem.at[spot], got_g.at[own * me + spot], **on(last)).start()
+
+        @pl.when(due & by_way)
+        def _():
+            pltpu.make_async_remote_copy(gout.at[spot], relay.at[spot], feed_g_sem.at[spot], got_relay.at[spot], **on(me - half)).start()
+
+        spot = t - 2 * own - own * (me + half)
+
+        @pl.when((me < edge) & (spot >= 0) & (spot < own))
+        def _():
+            arrival(relay, spot, got_relay).wait_recv()
+            c = own * (me + half) + spot
+            pltpu.make_async_remote_copy(relay.at[spot], g_all.at[c], relay_sem.at[spot], got_g.at[c], **on(last)).start()
+
     def store_copies(c):
         pairs = [(a_buf, a_all), (gp_buf, gp_all), (mid_buf, mid_all), (ab_buf, ab_all), (gpb_buf, gpb_all)]
         return [load(src, dst.at[c], st_sem.at[k]) for k, (src, dst) in enumerate(pairs)]
@@ -246,17 +292,8 @@
     def step(t, _):
         cf, cb = fwd_chunk(t), bwd_chunk(t)
         has_f, has_b = valid(cf), valid(cb)
-        fed = t + own - own * me
-
-        @pl.when((me != 0) & (fed >= 0) & (fed < own))
-        def _():
-            pltpu.make_async_remote_copy(acts.at[fed], h_all.at[own * me + fed], feed_h_sem.at[fed], got_h.at[own * me + fed], **on(0)).start()
-
-        fed_g = t - own * me
-
-        @pl.when((me != last) & (fed_g >= 0) & (fed_g < own))
-        def _():
-            pltpu.make_async_remote_copy(gout.at[fed_g], g_all.at[own * me + fed_g], feed_g_sem.at[fed_g], got_g.at[own * me + fed_g], **on(last)).start()
+        feed_acts(t)
+        feed_grads(t)
 
         @pl.when(valid(cf - 1))
         def _():
@@ -368,6 +405,10 @@
         def _():
             load(gout.at[k], gout.at[k], feed_g_sem.at[k]).wait()
             arrival(acts_out, k, got_out).wait_recv()
+
+        @pl.when((me < edge) | (me >= half + edge))
+        def _():
+            load(relay.at[k], relay.at[k], relay_sem.at[k]).wait()
         return 0
 
     lax.fori_loop(0, own, settle, 0)
@@ -385,7 +426,7 @@
     outs = [
         shape((own, ROWS, width), bf), shape((own, ROWS, width), bf),
         shape(ua.shape, f32), shape(wa.shape, f32), shape(ub.shape, f32), shape(wb.shape, f32),
-        shape((chunks, ROWS, width), bf), shape((chunks, ROWS, width), bf), shape((chunks, ROWS, width), bf),
+        shape((chunks, ROWS, width), bf), shape((chunks, ROWS, width), bf), shape((own, ROWS, width), bf), shape((chunks, ROWS, width), bf),
         shape((chunks, ROWS, wide), bf), shape((chunks, ROWS, wide), f32),
         shape((chunks, ROWS, narrow), bf), shape((chunks, ROWS, narrow), f32),
     ]
@@ -397,7 +438,7 @@
         vm(tok, bf), vm(wid, bf), vm(wid, f32), vm(tok, bf), vm(nar, bf), vm(nar, f32), vm((SLOTS,) + tok, bf),
         vm((2,) + tok, bf), vm((2,) + wid, f32), vm((2,) + nar, f32), vm(nar, bf), vm(tok, bf), vm(wid, bf), vm((SLOTS,) + tok, bf),
         vm(wid, bf), vm(tok, bf), vm(tok, bf), vm(nar, bf),
-        dma((chunks,)), dma((chunks,)), dma((own,)), dma((own,)), dma((SLOTS,)), dma((SLOTS,)), dma((own,)), dma((own,)),
+        dma((chunks,)), dma((chunks,)), dma((own,)), dma((own,)), dma((SLOTS,)), dma((SLOTS,)), dma((own,)), dma((own,)), dma((own,)), dma((own,)),
         dma, dma, dma((2,)), dma((2,)), dma((4,)), dma((5,)), dma((4,)),
     ]
     results = pl.pallas_call(

time: 910 us -> 897 us (0.986)
  Pallas kernels: 886 us -> 874 us
    pallas_call x1, Pallas kernels: 886 us -> 874 us  [run_stages(): pl.pallas_call(functools.partial(kernel, axis), out_shape=outs, in_specs=...]
where the time goes in v5:
time: 897 us; the launch traced here: 896 us
  Pallas kernels  874 us (97%)
  local copies, waits for them, and re-layouts  21.9 us (2%)
    pallas_call x1, Pallas kernels, run_stages(): pl.pallas_call(functools.partial(kernel, axis), out_shape=outs, in_specs=...  874 us
    unnamed x20, local copies, waits for them, and re-layouts  21.9 us

profile of v5, /device:TPU:0, one launch (start us, length us, event | category | flops | bytes accessed | tf_op | source)
XLA Modules:
  0.0 896.4 jit_solution(17078961151442751734)
XLA Ops:
  0.6 873.8 %shard_map.109 = (bf16[8,256,768]{2,1,0:T(8,128)(2,1)}, bf16[8,256,768]{2,1,0:T(8,128)(2,1)}, f32[768,3072]{1,0:T(8,128)}, f32[3072,768]{1,0:T(8,128)}, f32[768,...) custom-call(bf16[8,256,768]{2,1,0:T(8,128)(2,1)} %bitcast.20, ...), custom_call_target="tpu_custom_call" | custom-call | tf_op jit(solution)/shard_map/pallas_call | solution.py:444
  874.4 0.0 copy-start.1
  874.4 0.0 copy-start
  874.5 3.9 copy.18
  878.4 0.0 copy-done.1
  878.4 0.0 slice-start
  878.4 1.7 copy.19
  880.0 2.3 copy-done
  882.3 0.0 slice-start.1
  882.3 0.0 slice-start.2
  882.3 4.8 copy.20
  887.1 0.0 slice-done
  887.1 1.2 slice-done.1
  888.2 0.2 slice-done.2
  888.5 0.0 copy-start.3
  888.5 4.0 copy.21
  892.5 0.0 copy-done.3
  892.5 0.0 copy-start.2
  892.5 1.4 copy.22
  893.9 1.1 copy-done.2
  895.0 1.4 copy.23
  (1 shorter events, 0.0 us)
Async XLA Ops:
  874.4 3.9 copy-start.1
  874.4 7.8 copy-start
  878.4 8.7 slice-start
  882.3 6.0 slice-start.1
  882.3 6.2 slice-start.2
  888.5 4.0 copy-start.3
  892.5 2.5 copy-start.2

commit v6 on v5

--- a/solution.py
+++ b/solution.py
@@ -15,7 +15,6 @@
 GELU_K = 0.044715
 
 ROWS = 256
-HOP = 2
 LAG = 2
 SLOTS = 4
 WIDE_COLS = 512
@@ -134,18 +133,21 @@
     own = acts.shape[0]
     chunks = own * stages
 
-    def offset(stage):
-        return HOP * stage + stage // 2
-
-    span = offset(last)
+    def ahead(stage):
+        return stage + stage // 2
+
+    def behind(stage):
+        return 2 * stage + stage // 2
+
+    span = ahead(last) + LAG + behind(last)
 
     weights = (ua, wa, ub, wb)
 
     def fwd_chunk(t):
-        return t - offset(me)
+        return t - ahead(me)
 
     def bwd_chunk(t):
-        return t - 2 * span - LAG + offset(me)
+        return t - span + behind(me)
 
     def valid(c):
         return (c >= 0) & (c < chunks)
@@ -169,14 +171,16 @@
         def _():
             local = (me == 0) & (c < own)
 
+            side = lax.rem(c, 2)
+
             @pl.when(local)
             def _():
-                load(acts.at[lax.rem(c, own)], h_buf, h_sem).start()
+                load(acts.at[lax.rem(c, own)], h_buf.at[side], h_sem.at[side]).start()
 
             @pl.when(jnp.logical_not(local))
             def _():
                 arrival(h_all, c, got_h).wait_recv()
-                load(h_all.at[c], h_buf, h_sem).start()
+                load(h_all.at[c], h_buf.at[side], h_sem.at[side]).start()
 
     def fetch_slopes(c):
         @pl.when(valid(c))
@@ -238,7 +242,7 @@
 
     def feed_acts(t):
         by_way = (me >= edge) & first_half
-        lead = jnp.where(me == 1, own, jnp.where(by_way, 2 * own, own + own // 2))
+        lead = jnp.where(first_half, own * me, own + own // 2)
         spot = t + lead - own * me
         due = (me != 0) & (spot >= 0) & (spot < own)
 
@@ -250,7 +254,7 @@
         def _():
             pltpu.make_async_remote_copy(acts.at[spot], relay.at[spot], feed_h_sem.at[spot], got_relay.at[spot], **on(me + half)).start()
 
-        spot = t + own + own // 4 - own * (me - half)
+        spot = t - me - 1
 
         @pl.when((me >= half + edge) & (spot >= 0) & (spot < own))
         def _():
@@ -260,7 +264,7 @@
 
     def feed_grads(t):
         by_way = jnp.logical_not(first_half) & (me < half + edge)
-        spot = t - own // 2 - own * me
+        spot = t - jnp.where(by_way, 0, own // 2) - own * me
         due = (me != last) & (spot >= 0) & (spot < own)
 
         @pl.when(due & jnp.logical_not(by_way))
@@ -271,7 +275,7 @@
         def _():
             pltpu.make_async_remote_copy(gout.at[spot], relay.at[spot], feed_g_sem.at[spot], got_relay.at[spot], **on(me - half)).start()
 
-        spot = t - 2 * own - own * (me + half)
+        spot = t - own - own // 2 - own * (me + half)
 
         @pl.when((me < edge) & (spot >= 0) & (spot < own))
         def _():
@@ -279,9 +283,23 @@
             c = own * (me + half) + spot
             pltpu.make_async_remote_copy(relay.at[spot], g_all.at[c], relay_sem.at[spot], got_g.at[c], **on(last)).start()
 
-    def store_copies(c):
-        pairs = [(a_buf, a_all), (gp_buf, gp_all), (mid_buf, mid_all), (ab_buf, ab_all), (gpb_buf, gpb_all)]
+    def wide_saves(c):
+        pairs = [(a_buf, a_all), (gp_buf, gp_all), (mid_buf, mid_all)]
         return [load(src, dst.at[c], st_sem.at[k]) for k, (src, dst) in enumerate(pairs)]
+
+    def narrow_saves(c):
+        pairs = [(ab_buf, ab_all), (gpb_buf, gpb_all)]
+        return [load(src, dst.at[c], st_sem.at[k + 3]) for k, (src, dst) in enumerate(pairs)]
+
+    def start(copies):
+        for copy in copies:
+            copy.start()
+
+    def saved(c, copies):
+        @pl.when(valid(c))
+        def _():
+            for copy in copies(c):
+                copy.wait()
 
     fetch_h(fwd_chunk(0))
     for total in (dua, dwa, dub, dwb):
@@ -295,23 +313,32 @@
         feed_acts(t)
         feed_grads(t)
 
-        @pl.when(valid(cf - 1))
-        def _():
-            for copy in store_copies(cf - 1):
-                copy.wait()
+        f_alone = has_f & jnp.logical_not(has_b)
+        late = f_alone & (cb + 1 < 0)
+        saved(cf - 1, wide_saves)
+
+        @pl.when(jnp.logical_not(late))
+        def _():
+            saved(cf - 1, narrow_saves)
 
         fetch_slopes(cb + 1)
 
+        @pl.when(me == 0)
+        def _():
+            fetch_h(cf + 1)
+
         @pl.when(has_b)
         def _():
             fetch_weight_operands(cb)
 
         b_side = lax.rem(jnp.maximum(cb, 0), 2)
+        f_side = lax.rem(jnp.maximum(cf, 0), 2)
+        h_now = h_buf.at[f_side]
         g_now, gp_now, gpb_now = g_buf.at[b_side], gp_in.at[b_side], gpb_in.at[b_side]
         f_slot, b_slot = lax.rem(cf, SLOTS), lax.rem(cb, SLOTS)
 
         def f_begin():
-            load(h_buf, h_buf, h_sem).wait()
+            load(h_now, h_now, h_sem.at[f_side]).wait()
 
             @pl.when(cf >= SLOTS)
             def _():
@@ -320,12 +347,10 @@
         def f_tasks():
             def done(h):
                 f_send[f_slot] = h
-            return forward_tasks(h_buf, weights, (a_buf, gp_buf, mid_buf, ab_buf, gpb_buf), done)
+            return forward_tasks(h_now, weights, (a_buf, gp_buf, mid_buf, ab_buf, gpb_buf), done)
 
         def f_end():
             send(f_send.at[f_slot], f_sem.at[f_slot], cf, me != last, me + 1, h_all, got_h, acts_out, got_out)
-            for copy in store_copies(cf):
-                copy.start()
 
         def b_begin():
             load(g_buf.at[0], g_buf.at[0], g_sem).wait()
@@ -351,12 +376,21 @@
             run_tasks(FB_ORDER, f_tasks() | b_tasks())
             b_end()
             f_end()
-
-        @pl.when(has_f & jnp.logical_not(has_b))
-        def _():
+            start(wide_saves(cf) + narrow_saves(cf))
+
+        @pl.when(f_alone)
+        def _():
+            tasks = f_tasks()
             f_begin()
-            run_tasks(F_ORDER, f_tasks())
+            run_tasks(F_ORDER[:-2], tasks)
+            start(wide_saves(cf))
+
+            @pl.when(late)
+            def _():
+                saved(cf - 1, narrow_saves)
+            run_tasks(F_ORDER[-2:], tasks)
             f_end()
+            start(narrow_saves(cf))
 
         @pl.when(has_b & jnp.logical_not(has_f))
         def _():
@@ -369,7 +403,10 @@
         @pl.when(steady)
         def _():
             fetch_g(cb + 1)
-            fetch_h(cf + 1)
+
+            @pl.when(me != 0)
+            def _():
+                fetch_h(cf + 1)
 
         @pl.when(has_b)
         def _():
@@ -385,7 +422,7 @@
             fetch_g(cb + 1)
         return 0
 
-    lax.fori_loop(0, chunks + 2 * span + LAG, step, 0)
+    lax.fori_loop(0, chunks + span, step, 0)
 
     finals = [load(src, dst, param_sem.at[k]) for k, (src, dst) in enumerate(
         [(dua, dua_hbm), (dwa, dwa_hbm), (dub, dub_hbm), (dwb, dwb_hbm)])]
@@ -435,11 +472,11 @@
     scratch = [
         vm(ua.shape, bf), vm(wa.shape, bf), vm(ub.shape, bf), vm(wb.shape, bf),
         vm(ua.shape, f32), vm(wa.shape, f32), vm(ub.shape, f32), vm(wb.shape, f32),
-        vm(tok, bf), vm(wid, bf), vm(wid, f32), vm(tok, bf), vm(nar, bf), vm(nar, f32), vm((SLOTS,) + tok, bf),
+        vm((2,) + tok, bf), vm(wid, bf), vm(wid, f32), vm(tok, bf), vm(nar, bf), vm(nar, f32), vm((SLOTS,) + tok, bf),
         vm((2,) + tok, bf), vm((2,) + wid, f32), vm((2,) + nar, f32), vm(nar, bf), vm(tok, bf), vm(wid, bf), vm((SLOTS,) + tok, bf),
         vm(wid, bf), vm(tok, bf), vm(tok, bf), vm(nar, bf),
         dma((chunks,)), dma((chunks,)), dma((own,)), dma((own,)), dma((SLOTS,)), dma((SLOTS,)), dma((own,)), dma((own,)), dma((own,)), dma((own,)),
-        dma, dma, dma((2,)), dma((2,)), dma((4,)), dma((5,)), dma((4,)),
+        dma((2,)), dma, dma((2,)), dma((2,)), dma((4,)), dma((5,)), dma((4,)),
     ]
     results = pl.pallas_call(
         functools.partial(kernel, axis),

time: 897 us -> 878 us (0.979)
  Pallas kernels: 874 us -> 854 us
    pallas_call x1, Pallas kernels: 874 us -> 854 us  [run_stages(): pl.pallas_call(functools.partial(kernel, axis), out_shape=outs, in_specs=...]
where the time goes in v6:
time: 878 us; the launch traced here: 877 us
  Pallas kernels  854 us (97%)
  local copies, waits for them, and re-layouts  21.9 us (2%)
    pallas_call x1, Pallas kernels, run_stages(): pl.pallas_call(functools.partial(kernel, axis), out_shape=outs, in_specs=...  854 us
    unnamed x20, local copies, waits for them, and re-layouts  21.9 us

profile of v6, /device:TPU:0, one launch (start us, length us, event | category | flops | bytes accessed | tf_op | source)
XLA Modules:
  0.0 876.6 jit_solution(16287231068183966762)
XLA Ops:
  0.6 854.0 %shard_map.109 = (bf16[8,256,768]{2,1,0:T(8,128)(2,1)}, bf16[8,256,768]{2,1,0:T(8,128)(2,1)}, f32[768,3072]{1,0:T(8,128)}, f32[3072,768]{1,0:T(8,128)}, f32[768,...) custom-call(bf16[8,256,768]{2,1,0:T(8,128)(2,1)} %bitcast.20, ...), custom_call_target="tpu_custom_call" | custom-call | tf_op jit(solution)/shard_map/pallas_call | solution.py:481
  854.6 0.0 copy-start.1
  854.6 0.0 copy-start
  854.6 3.9 copy.18
  858.6 0.0 copy-done.1
  858.6 0.0 slice-start
  858.6 1.7 copy.19
  860.2 2.3 copy-done
  862.5 0.0 slice-start.1
  862.5 0.0 slice-start.2
  862.5 4.8 copy.20
  867.3 0.0 slice-done
  867.3 1.2 slice-done.1
  868.4 0.2 slice-done.2
  868.7 0.0 copy-start.3
  868.7 4.0 copy.21
  872.7 0.0 copy-done.3
  872.7 0.0 copy-start.2
  872.7 1.4 copy.22
  874.1 1.1 copy-done.2
  875.2 1.4 copy.23
  (1 shorter events, 0.0 us)
Async XLA Ops:
  854.6 3.9 copy-start.1
  854.6 7.8 copy-start
  858.6 8.7 slice-start
  862.5 6.0 slice-start.1
  862.5 6.2 slice-start.2
  868.7 4.0 copy-start.3
  872.7 2.5 copy-start.2

commit v7 on v6

--- a/solution.py
+++ b/solution.py
@@ -162,6 +162,9 @@
         [(ua_hbm, ua), (wa_hbm, wa), (ub_hbm, ub), (wb_hbm, wb)])]
     for copy in params:
         copy.start()
+    barrier = pltpu.get_barrier_semaphore()
+    for device in range(stages):
+        pl.semaphore_signal(barrier, inc=1, **on(device))
 
     def arrival(buf, c, sem):
         return pltpu.make_async_remote_copy(buf.at[c], buf.at[c], sem.at[c], sem.at[c], **on(me))
@@ -263,7 +266,7 @@
             pltpu.make_async_remote_copy(relay.at[spot], h_all.at[c], relay_sem.at[spot], got_h.at[c], **on(0)).start()
 
     def feed_grads(t):
-        by_way = jnp.logical_not(first_half) & (me < half + edge)
+        by_way = (me == 0) | (jnp.logical_not(first_half) & (me < half + edge))
         spot = t - jnp.where(by_way, 0, own // 2) - own * me
         due = (me != last) & (spot >= 0) & (spot < own)
 
@@ -273,14 +276,15 @@
 
         @pl.when(due & by_way)
         def _():
-            pltpu.make_async_remote_copy(gout.at[spot], relay.at[spot], feed_g_sem.at[spot], got_relay.at[spot], **on(me - half)).start()
-
-        spot = t - own - own // 2 - own * (me + half)
-
-        @pl.when((me < edge) & (spot >= 0) & (spot < own))
+            pltpu.make_async_remote_copy(gout.at[spot], relay.at[spot], feed_g_sem.at[spot], got_relay.at[spot], **on(lax.rem(me + half, stages))).start()
+
+        source = jnp.where(me == half, 0, me + half)
+        spot = t - jnp.where(me == half, ahead(half), own + own // 2 + own * source)
+
+        @pl.when(((me < edge) | (me == half)) & (spot >= 0) & (spot < own))
         def _():
             arrival(relay, spot, got_relay).wait_recv()
-            c = own * (me + half) + spot
+            c = own * source + spot
             pltpu.make_async_remote_copy(relay.at[spot], g_all.at[c], relay_sem.at[spot], got_g.at[c], **on(last)).start()
 
     def wide_saves(c):
@@ -301,9 +305,12 @@
             for copy in copies(c):
                 copy.wait()
 
-    fetch_h(fwd_chunk(0))
+    @pl.when(me == 0)
+    def _():
+        load(acts.at[0], h_buf.at[0], h_sem.at[0]).start()
     for total in (dua, dwa, dub, dwb):
         total[...] = jnp.zeros_like(total)
+    pl.semaphore_wait(barrier, stages)
     for copy in params:
         copy.wait()
 
@@ -443,7 +450,7 @@
             load(gout.at[k], gout.at[k], feed_g_sem.at[k]).wait()
             arrival(acts_out, k, got_out).wait_recv()
 
-        @pl.when((me < edge) | (me >= half + edge))
+        @pl.when((me < edge) | (me == half) | (me >= half + edge))
         def _():
             load(relay.at[k], relay.at[k], relay_sem.at[k]).wait()
         return 0
@@ -484,7 +491,7 @@
         in_specs=[ANY] * 6,
         out_specs=[ANY] * len(outs),
         scratch_shapes=scratch,
-        compiler_params=pltpu.CompilerParams(vmem_limit_bytes=VMEM_LIMIT, has_side_effects=True),
+        compiler_params=pltpu.CompilerParams(vmem_limit_bytes=VMEM_LIMIT, has_side_effects=True, collective_id=0),
     )(acts.reshape(own, ROWS, width), gout.reshape(own, ROWS, width), ua, wa, ub, wb)
     return results[:6]
 

time: 878 us -> 858 us (0.977)
  Pallas kernels: 854 us -> 834 us
    pallas_call x1, Pallas kernels: 854 us -> 834 us  [run_stages(): pl.pallas_call(functools.partial(kernel, axis), out_shape=outs, in_specs=...]
where the time goes in v7:
time: 858 us; the launch traced here: 857 us
  Pallas kernels  834 us (97%)
  local copies, waits for them, and re-layouts  21.9 us (3%)
    pallas_call x1, Pallas kernels, run_stages(): pl.pallas_call(functools.partial(kernel, axis), out_shape=outs, in_specs=...  834 us
    unnamed x20, local copies, waits for them, and re-layouts  21.9 us

profile of v7, /device:TPU:0, one launch (start us, length us, event | category | flops | bytes accessed | tf_op | source)
XLA Modules:
  0.0 856.9 jit_solution(5872727950887982026)
XLA Ops:
  0.6 834.3 %shard_map.109 = (bf16[8,256,768]{2,1,0:T(8,128)(2,1)}, bf16[8,256,768]{2,1,0:T(8,128)(2,1)}, f32[768,3072]{1,0:T(8,128)}, f32[3072,768]{1,0:T(8,128)}, f32[768,...) custom-call(bf16[8,256,768]{2,1,0:T(8,128)(2,1)} %bitcast.20, ...), custom_call_target="tpu_custom_call" | custom-call | tf_op jit(solution)/shard_map/pallas_call | solution.py:488
  834.9 0.0 copy-start.1
  834.9 0.0 copy-start
  834.9 3.9 copy.18
  838.8 0.0 copy-done.1
  838.8 0.0 slice-start
  838.8 1.7 copy.19
  840.5 2.3 copy-done
  842.8 0.0 slice-start.1
  842.8 0.0 slice-start.2
  842.8 4.8 copy.20
  847.6 0.0 slice-done
  847.6 1.2 slice-done.1
  848.7 0.2 slice-done.2
  849.0 0.0 copy-start.3
  849.0 4.0 copy.21
  852.9 0.0 copy-done.3
  852.9 0.0 copy-start.2
  852.9 1.4 copy.22
  854.3 1.1 copy-done.2
  855.4 1.4 copy.23
  (1 shorter events, 0.0 us)
Async XLA Ops:
  834.9 3.9 copy-start.1
  834.9 7.8 copy-start
  838.8 8.7 %slice-start = ((s8[9437184]{0:T(1024)(128)(4,1)}), s8[4194304]{0:T(1024)(128)(4,1)S(1)}, s32[]{:S(2)}) async-start(s8[9437184]{0:T(1024)(128)(4,1)} %bitcast.12), calls=%async_computation | async-start | bytes 8388608
  842.8 6.0 slice-start.1
  842.8 6.2 slice-start.2
  849.0 4.0 copy-start.3
  852.9 2.5 copy-start.2

commit v8 on v7

--- a/solution.py
+++ b/solution.py
@@ -16,10 +16,13 @@
 
 ROWS = 256
 LAG = 2
+FIRST = 5
 SLOTS = 4
 WIDE_COLS = 512
 F_ORDER = 'zzczczczczccyo'
+HALF_ORDER = 'zzczczczczccyo'
 B_ORDER = 'dmxxpxpxpxpxpp'
+
 FB_ORDER = 'zdmzxzcxpzcxpzcxpzccpxcxpypo'
 
 NT = (((1,), (1,)), ((), ()))
@@ -124,7 +127,7 @@
     h_buf, a_buf, gp_buf, mid_buf, ab_buf, gpb_buf, f_send,
     g_buf, gp_in, gpb_in, dzb_buf, gmid_buf, dz_buf, b_send,
     a_in, h_in, mid_in, ab_in,
-    got_h, got_g, got_out, got_gin, f_sem, b_sem, feed_h_sem, feed_g_sem, got_relay, relay_sem,
+    got_h, got_g, got_out, got_gin, f_sem, b_sem, feed_h_sem, feed_g_sem, got_relay, relay_sem, half_sem, keep_sem, half_st_sem,
     h_sem, g_sem, gp_sem, gpb_sem, w_sem, st_sem, param_sem,
 ):
     me = lax.axis_index(axis)
@@ -169,21 +172,41 @@
     def arrival(buf, c, sem):
         return pltpu.make_async_remote_copy(buf.at[c], buf.at[c], sem.at[c], sem.at[c], **on(me))
 
+    halved = jnp.where(me == last, LAG, FIRST)
+
+    def h_slot(c):
+        return jnp.where(c < FIRST, 2 + jnp.maximum(c, 0), lax.rem(jnp.maximum(c, 0), 2))
+
+    def half_rows(r):
+        return pl.ds(pl.multiple_of(r * (ROWS // 2), ROWS // 2), ROWS // 2)
+
+    def half_arrival(c, r):
+        buf = h_buf.at[h_slot(c), half_rows(r)]
+        return pltpu.make_async_remote_copy(buf, buf, half_sem.at[c, r], half_sem.at[c, r], **on(me))
+
+    def keep_copy(c):
+        return load(h_buf.at[h_slot(c)], h_all.at[c], keep_sem.at[c])
+
+    def half_saves(c, r):
+        pairs = [(a_buf, a_all), (gp_buf, gp_all), (mid_buf, mid_all), (ab_buf, ab_all), (gpb_buf, gpb_all)]
+        return [load(src.at[half_rows(r)], dst.at[c, half_rows(r)], half_st_sem.at[r, k]) for k, (src, dst) in enumerate(pairs)]
+
     def fetch_h(c):
-        @pl.when(valid(c))
+        @pl.when(valid(c) & ((c >= FIRST) | (me == 0)))
         def _():
             local = (me == 0) & (c < own)
 
             side = lax.rem(c, 2)
+            buf = h_buf.at[h_slot(c)]
 
             @pl.when(local)
             def _():
-                load(acts.at[lax.rem(c, own)], h_buf.at[side], h_sem.at[side]).start()
+                load(acts.at[lax.rem(c, own)], buf, h_sem.at[side]).start()
 
             @pl.when(jnp.logical_not(local))
             def _():
                 arrival(h_all, c, got_h).wait_recv()
-                load(h_all.at[c], h_buf.at[side], h_sem.at[side]).start()
+                load(h_all.at[c], buf, h_sem.at[side]).start()
 
     def fetch_slopes(c):
         @pl.when(valid(c))
@@ -192,11 +215,17 @@
             load(gp_all.at[c], gp_in.at[side], gp_sem.at[side]).start()
             load(gpb_all.at[c], gpb_in.at[side], gpb_sem.at[side]).start()
 
+    def g_slot(c):
+        return jnp.where(c == chunks - 1, 2, lax.rem(jnp.maximum(c, 0), 2))
+
+    def comes_direct(c):
+        return (c == chunks - 1) & (me != last)
+
     def fetch_g(c):
-        @pl.when(valid(c))
+        @pl.when(valid(c) & jnp.logical_not(comes_direct(c)))
         def _():
             local = (me == last) & (c >= chunks - own)
-            buf = g_buf.at[lax.rem(c, 2)]
+            buf = g_buf.at[g_slot(c)]
 
             @pl.when(local)
             def _():
@@ -245,8 +274,8 @@
 
     def feed_acts(t):
         by_way = (me >= edge) & first_half
-        lead = jnp.where(first_half, own * me, own + own // 2)
-        spot = t + lead - own * me
+        later = jnp.where(me < half + edge, own * me - own - own // 2, 3 * own + 3 + own * (me - half - edge))
+        spot = t - jnp.where(first_half, 0, later)
         due = (me != 0) & (spot >= 0) & (spot < own)
 
         @pl.when(due & jnp.logical_not(by_way))
@@ -257,7 +286,7 @@
         def _():
             pltpu.make_async_remote_copy(acts.at[spot], relay.at[spot], feed_h_sem.at[spot], got_relay.at[spot], **on(me + half)).start()
 
-        spot = t - me - 1
+        spot = t - me - 4
 
         @pl.when((me >= half + edge) & (spot >= 0) & (spot < own))
         def _():
@@ -267,7 +296,8 @@
 
     def feed_grads(t):
         by_way = (me == 0) | (jnp.logical_not(first_half) & (me < half + edge))
-        spot = t - jnp.where(by_way, 0, own // 2) - own * me
+        later = jnp.where(me == 1, 2 * own + 2, own // 2 + own * me)
+        spot = t - jnp.where(me == 0, 0, jnp.where(by_way, 2 * own - 2 + 10 * (me - half), later))
         due = (me != last) & (spot >= 0) & (spot < own)
 
         @pl.when(due & jnp.logical_not(by_way))
@@ -279,9 +309,11 @@
             pltpu.make_async_remote_copy(gout.at[spot], relay.at[spot], feed_g_sem.at[spot], got_relay.at[spot], **on(lax.rem(me + half, stages))).start()
 
         source = jnp.where(me == half, 0, me + half)
-        spot = t - jnp.where(me == half, ahead(half), own + own // 2 + own * source)
-
-        @pl.when(((me < edge) | (me == half)) & (spot >= 0) & (spot < own))
+        early = jnp.maximum(t - ahead(half), -1)
+        spot = jnp.where(me == half, jnp.where(early < own - 1, (early + 1) // 2, early - own // 2 + 1), t - span - own * me)
+        due = (me < edge) | ((me == half) & (early >= 0) & ((early >= own - 1) | (lax.rem(early + 2, 2) == 0)))
+
+        @pl.when(due & (spot >= 0) & (spot < own))
         def _():
             arrival(relay, spot, got_relay).wait_recv()
             c = own * source + spot
@@ -307,7 +339,7 @@
 
     @pl.when(me == 0)
     def _():
-        load(acts.at[0], h_buf.at[0], h_sem.at[0]).start()
+        load(acts.at[0], h_buf.at[h_slot(0)], h_sem.at[0]).start()
     for total in (dua, dwa, dub, dwb):
         total[...] = jnp.zeros_like(total)
     pl.semaphore_wait(barrier, stages)
@@ -322,11 +354,27 @@
 
         f_alone = has_f & jnp.logical_not(has_b)
         late = f_alone & (cb + 1 < 0)
-        saved(cf - 1, wide_saves)
-
-        @pl.when(jnp.logical_not(late))
-        def _():
-            saved(cf - 1, narrow_saves)
+        before = cf - 1
+        before_halved = valid(before) & (before < halved)
+        loose = (cf < halved) & (cb + 1 < 0)
+
+        @pl.when(valid(before) & (before >= halved))
+        def _():
+            saved(before, wide_saves)
+
+            @pl.when(jnp.logical_not(late))
+            def _():
+                saved(before, narrow_saves)
+
+        @pl.when(before_halved & jnp.logical_not(loose))
+        def _():
+            for r in range(2):
+                for copy in half_saves(before, r):
+                    copy.wait()
+
+        @pl.when(valid(before) & (before < FIRST) & (me != 0))
+        def _():
+            keep_copy(before).wait()
 
         fetch_slopes(cb + 1)
 
@@ -340,12 +388,22 @@
 
         b_side = lax.rem(jnp.maximum(cb, 0), 2)
         f_side = lax.rem(jnp.maximum(cf, 0), 2)
-        h_now = h_buf.at[f_side]
-        g_now, gp_now, gpb_now = g_buf.at[b_side], gp_in.at[b_side], gpb_in.at[b_side]
+        h_now = h_buf.at[h_slot(cf)]
+        g_now, gp_now, gpb_now = g_buf.at[g_slot(cb)], gp_in.at[b_side], gpb_in.at[b_side]
         f_slot, b_slot = lax.rem(cf, SLOTS), lax.rem(cb, SLOTS)
 
         def f_begin():
-            load(h_now, h_now, h_sem.at[f_side]).wait()
+            direct = (cf < FIRST) & (me != 0)
+
+            @pl.when(direct)
+            def _():
+                for r in range(2):
+                    half_arrival(cf, r).wait_recv()
+                keep_copy(cf).start()
+
+            @pl.when(jnp.logical_not(direct))
+            def _():
+                load(h_now, h_now, h_sem.at[f_side]).wait()
 
             @pl.when(cf >= SLOTS)
             def _():
@@ -360,7 +418,13 @@
             send(f_send.at[f_slot], f_sem.at[f_slot], cf, me != last, me + 1, h_all, got_h, acts_out, got_out)
 
         def b_begin():
-            load(g_buf.at[0], g_buf.at[0], g_sem).wait()
+            @pl.when(comes_direct(cb))
+            def _():
+                pltpu.make_async_remote_copy(g_now, g_now, got_g.at[chunks - 1], got_g.at[chunks - 1], **on(me)).wait_recv()
+
+            @pl.when(jnp.logical_not(comes_direct(cb)))
+            def _():
+                load(g_now, g_now, g_sem).wait()
             load(gp_now, gp_now, gp_sem.at[b_side]).wait()
             load(gpb_now, gpb_now, gpb_sem.at[b_side]).wait()
 
@@ -374,6 +438,15 @@
             return backward_tasks(g_now, weights, (gp_now, gpb_now), (dzb_buf, gmid_buf, dz_buf), done)
 
         def b_end():
+            @pl.when((cb == chunks - 1) & (me != 0))
+            def _():
+                pltpu.make_async_remote_copy(b_send.at[b_slot], g_buf.at[2], b_sem.at[b_slot], got_g.at[chunks - 1], **on(me - 1)).start()
+
+            @pl.when((cb != chunks - 1) | (me == 0))
+            def _():
+                send_back()
+
+        def send_back():
             send(b_send.at[b_slot], b_sem.at[b_slot], cb, me != 0, me - 1, g_all, got_g, grad_in, got_gin)
 
         @pl.when(has_f & has_b)
@@ -385,16 +458,59 @@
             f_end()
             start(wide_saves(cf) + narrow_saves(cf))
 
-        @pl.when(f_alone)
+        @pl.when(has_f & (cf < halved))
+        def _():
+            @pl.when(me == 0)
+            def _():
+                load(h_now, h_now, h_sem.at[f_side]).wait()
+
+            @pl.when(cf >= SLOTS)
+            def _():
+                sent(f_send.at[f_slot], f_sem.at[f_slot])
+
+            def half_chunk(r, _):
+                rows = half_rows(r)
+                h_half, out_half = h_now.at[rows], f_send.at[f_slot, rows]
+
+                @pl.when(me != 0)
+                def _():
+                    half_arrival(cf, r).wait_recv()
+
+                    @pl.when(r == 1)
+                    def _():
+                        keep_copy(cf).start()
+
+                @pl.when(before_halved & loose)
+                def _():
+                    for copy in half_saves(before, r):
+                        copy.wait()
+
+                def done(h):
+                    out_half[...] = h
+                run_tasks(HALF_ORDER, forward_tasks(h_half, weights, [buf.at[rows] for buf in (a_buf, gp_buf, mid_buf, ab_buf, gpb_buf)], done))
+
+                @pl.when(me != last)
+                def _():
+                    pltpu.make_async_remote_copy(out_half, h_half, f_sem.at[f_slot], half_sem.at[cf, r], **on(me + 1)).start()
+
+                @pl.when(me == last)
+                def _():
+                    pltpu.make_async_remote_copy(out_half, acts_out.at[cf, rows], f_sem.at[f_slot], got_out.at[cf], **on(0)).start()
+                start(half_saves(cf, r))
+                return 0
+
+            lax.fori_loop(0, 2, half_chunk, 0)
+
+        @pl.when(f_alone & (cf >= halved))
         def _():
             tasks = f_tasks()
             f_begin()
             run_tasks(F_ORDER[:-2], tasks)
             start(wide_saves(cf))
 
-            @pl.when(late)
-            def _():
-                saved(cf - 1, narrow_saves)
+            @pl.when(late & (before >= halved))
+            def _():
+                saved(before, narrow_saves)
             run_tasks(F_ORDER[-2:], tasks)
             f_end()
             start(narrow_saves(cf))
@@ -405,7 +521,7 @@
             run_tasks(B_ORDER, b_tasks())
             b_end()
 
-        steady = valid(cf + 1)
+        steady = cb + 1 < chunks - 2
 
         @pl.when(steady)
         def _():
@@ -479,10 +595,10 @@
     scratch = [
         vm(ua.shape, bf), vm(wa.shape, bf), vm(ub.shape, bf), vm(wb.shape, bf),
         vm(ua.shape, f32), vm(wa.shape, f32), vm(ub.shape, f32), vm(wb.shape, f32),
-        vm((2,) + tok, bf), vm(wid, bf), vm(wid, f32), vm(tok, bf), vm(nar, bf), vm(nar, f32), vm((SLOTS,) + tok, bf),
-        vm((2,) + tok, bf), vm((2,) + wid, f32), vm((2,) + nar, f32), vm(nar, bf), vm(tok, bf), vm(wid, bf), vm((SLOTS,) + tok, bf),
+        vm((2 + FIRST,) + tok, bf), vm(wid, bf), vm(wid, f32), vm(tok, bf), vm(nar, bf), vm(nar, f32), vm((SLOTS,) + tok, bf),
+        vm((3,) + tok, bf), vm((2,) + wid, f32), vm((2,) + nar, f32), vm(nar, bf), vm(tok, bf), vm(wid, bf), vm((SLOTS,) + tok, bf),
         vm(wid, bf), vm(tok, bf), vm(tok, bf), vm(nar, bf),
-        dma((chunks,)), dma((chunks,)), dma((own,)), dma((own,)), dma((SLOTS,)), dma((SLOTS,)), dma((own,)), dma((own,)), dma((own,)), dma((own,)),
+        dma((chunks,)), dma((chunks,)), dma((own,)), dma((own,)), dma((SLOTS,)), dma((SLOTS,)), dma((own,)), dma((own,)), dma((own,)), dma((own,)), dma((FIRST, 2)), dma((FIRST,)), dma((2, 5)),
         dma((2,)), dma, dma((2,)), dma((2,)), dma((4,)), dma((5,)), dma((4,)),
     ]
     results = pl.pallas_call(

time: 858 us -> 854 us (level)
  no operation moved by 1% of the time
where the time goes in v8:
time: 854 us
  Pallas kernels  831 us (97%)
  local copies, waits for them, and re-layouts  21.9 us (3%)
    pallas_call x1, Pallas kernels, run_stages(): pl.pallas_call(functools.partial(kernel, axis), out_shape=outs, in_specs=...  831 us
    unnamed x20, local copies, waits for them, and re-layouts  21.9 us

profile of v8, /device:TPU:0, one launch (start us, length us, event | category | flops | bytes accessed | tf_op | source)
XLA Modules:
  0.0 853.6 jit_solution(4314672025395083820)
XLA Ops:
  0.6 831.0 %shard_map.109 = (bf16[8,256,768]{2,1,0:T(8,128)(2,1)}, bf16[8,256,768]{2,1,0:T(8,128)(2,1)}, f32[768,3072]{1,0:T(8,128)}, f32[3072,768]{1,0:T(8,128)}, f32[768,...) custom-call(bf16[8,256,768]{2,1,0:T(8,128)(2,1)} %bitcast.20, ...), custom_call_target="tpu_custom_call" | custom-call | tf_op jit(solution)/shard_map/pallas_call | solution.py:604
  831.6 0.0 copy-start.1
  831.6 0.0 copy-start
  831.6 3.9 copy.18
  835.5 0.0 copy-done.1
  835.6 0.0 slice-start
  835.6 1.7 copy.19
  837.2 2.3 copy-done
  839.5 0.0 slice-start.1
  839.5 0.0 slice-start.2
  839.5 4.8 copy.20
  844.3 0.0 slice-done
  844.3 1.2 slice-done.1
  845.4 0.2 slice-done.2
  845.7 0.0 copy-start.3
  845.7 4.0 copy.21
  849.6 0.0 copy-done.3
  849.6 0.0 copy-start.2
  849.6 1.4 copy.22
  851.1 1.1 copy-done.2
  852.2 1.4 copy.23
  (1 shorter events, 0.0 us)
Async XLA Ops:
  831.6 3.9 copy-start.1
  831.6 7.8 copy-start
  835.6 8.7 %slice-start = ((s8[9437184]{0:T(1024)(128)(4,1)}), s8[4194304]{0:T(1024)(128)(4,1)S(1)}, s32[]{:S(2)}) async-start(s8[9437184]{0:T(1024)(128)(4,1)} %bitcast.12), calls=%async_computation | async-start | bytes 8388608
  839.5 6.0 slice-start.1
  839.5 6.2 slice-start.2
  845.7 4.0 copy-start.3
  849.6 2.5 copy-start.2

commit v9 on v8

--- a/solution.py
+++ b/solution.py
@@ -23,7 +23,7 @@
 HALF_ORDER = 'zzczczczczccyo'
 B_ORDER = 'dmxxpxpxpxpxpp'
 
-FB_ORDER = 'zdmzxzcxpzcxpzcxpzccpxcxpypo'
+FB_ORDER = 'zdmzxzcxpzcpxzcxpzccpxcxpypo'
 
 NT = (((1,), (1,)), ((), ()))
 TN = (((0,), (0,)), ((), ()))

time: 854 us -> 850 us (level)
  no operation moved by 1% of the time
where the time goes in v9:
time: 850 us; the launch traced here: 849 us
  Pallas kernels  826 us (97%)
  local copies, waits for them, and re-layouts  21.9 us (3%)
    pallas_call x1, Pallas kernels, run_stages(): pl.pallas_call(functools.partial(kernel, axis), out_shape=outs, in_specs=...  826 us
    unnamed x20, local copies, waits for them, and re-layouts  21.9 us

profile of v9, /device:TPU:0, one launch (start us, length us, event | category | flops | bytes accessed | tf_op | source)
XLA Modules:
  0.0 848.9 jit_solution(5086084067595851026)
XLA Ops:
  0.6 826.3 %shard_map.109 = (bf16[8,256,768]{2,1,0:T(8,128)(2,1)}, bf16[8,256,768]{2,1,0:T(8,128)(2,1)}, f32[768,3072]{1,0:T(8,128)}, f32[3072,768]{1,0:T(8,128)}, f32[768,...) custom-call(bf16[8,256,768]{2,1,0:T(8,128)(2,1)} %bitcast.20, ...), custom_call_target="tpu_custom_call" | custom-call | tf_op jit(solution)/shard_map/pallas_call | solution.py:604
  826.9 0.0 copy-start.1
  826.9 0.0 copy-start
  826.9 3.9 copy.18
  830.8 0.0 copy-done.1
  830.8 0.0 slice-start
  830.8 1.7 copy.19
  832.5 2.3 copy-done
  834.8 0.0 slice-start.1
  834.8 0.0 slice-start.2
  834.8 4.8 copy.20
  839.6 0.0 slice-done
  839.6 1.2 slice-done.1
  840.7 0.2 slice-done.2
  841.0 0.0 copy-start.3
  841.0 4.0 copy.21
  844.9 0.0 copy-done.3
  844.9 0.0 copy-start.2
  844.9 1.4 copy.22
  846.3 1.1 copy-done.2
  847.4 1.4 copy.23
  (1 shorter events, 0.0 us)
Async XLA Ops:
  826.9 3.9 copy-start.1
  826.9 7.8 copy-start
  830.8 8.7 %slice-start = ((s8[9437184]{0:T(1024)(128)(4,1)}), s8[4194304]{0:T(1024)(128)(4,1)S(1)}, s32[]{:S(2)}) async-start(s8[9437184]{0:T(1024)(128)(4,1)} %bitcast.12), calls=%async_computation | async-start | bytes 8388608
  834.8 6.0 slice-start.1
  834.8 6.2 slice-start.2
  841.0 4.0 copy-start.3
  844.9 2.5 copy-start.2
